TPU v7x, 32 devices: a whole 2x2x4 slice. The times are simulated.
32 devices in a mesh: gene: 4 (over y, x), prot: 8 (over z, core).
Axes of the slice: x: 2, y: 2, z: 4, core: 2. Of those that a mesh axis runs over, the one named last changes fastest.
Arguments:
- density: float32 [256, 48, 16, 128], P('gene', 'prot'), may hold values from 0 to 2
- levels: float32 [8], replicated, may hold values from 0.1 to 0.9
- rate_index: int32 [256, 3], P('gene'), may hold values from 0 to 7
- on_rate: float32 [8], replicated, may hold values from 0.2 to 3
- off_rate: float32 [8], replicated, may hold values from 0.2 to 3
- gene_order: int32 [4], replicated, may hold values from 0 to 3, each once
Outputs:
- evolved: float32 [256, 48, 16, 128], P('gene', 'prot')
Inputs may be any that keep to these rules, and one draw needn't show every extreme that they name: `gene_order`: a permutation of 0 to 3.
All inputs are finite; a program needn't handle non-finite values.
Results may differ from a plain program's by a relative error of at most 0.00002.
Values sent between devices are 32-bit elements; how exact they have to be, the bound alone decides.
A program may use at most 128 MiB of HBM per device.

v0:
```python
from functools import partial

import jax
import jax.numpy as jnp
from jax import lax
from jax.experimental import pallas as pl
from jax.experimental.pallas import tpu as pltpu
from jax.sharding import PartitionSpec as P

STATE_BITS = 8
BLOCKS = 4
SUBSTEPS = 6
DIFF = 1.0
TIME_STEP = 0.15
TOP = 2**BLOCKS
GROUP = 4
CHUNK = 8
MESH = pl.DeviceIdType.MESH


class Plan:
    def __init__(self, genes, prots, count, width, size_y, size_z):
        self.genes, self.prots = genes, prots
        self.units = count * genes // TOP
        self.mids = count // self.units
        self.split = self.units // genes
        self.slabs = prots // self.split
        self.width, self.size_y, self.size_z = width, size_y, size_z
        self.cells = width * self.split
        self.total_x = width * prots
        self.halo = SUBSTEPS
        self.first = self.halo + 2
        self.layers = self.cells + 2 * self.first
        assert self.split * genes == self.units and self.slabs * self.split == prots
        assert self.cells >= self.halo
        gene_bits = genes.bit_length() - 1
        self.masks = [
            1 << (gene_bits - 1 - k) if k < gene_bits else 1 << (BLOCKS - 1 - (k - gene_bits))
            for k in range(BLOCKS)
        ]


def body(
    pn, x_ref, rate_ref, levels_ref, on_ref, off_ref, order_ref, out_ref,
    buf, land, tab_u, tab_d, tab_y, tab_z, tab_s, shift, pair,
    in_send, in_recv, out_send, out_recv, halo_send, halo_recv,
):
    g, p = lax.axis_index("gene"), lax.axis_index("prot")
    ny = pn.size_y
    q, r = p // pn.slabs, p % pn.slabs
    unit = g * pn.split + q
    part, sub = p // pn.split, p % pn.split
    home = jnp.logical_and(part == r, True)
    has_left, has_right = r > 0, r < pn.slabs - 1

    def rows(layer, n):
        return pl.ds(pl.multiple_of(layer * ny, ny), n * ny)

    def unit_of(k):
        return lax.rem(unit + k, pn.units)

    def in_target(u):
        return (u // pn.split, (u % pn.split) * pn.slabs + part)

    def source_of(k):
        return lax.rem(g * pn.split + sub + k, pn.units)

    def out_target(u):
        return (u // pn.split, r * pn.split + u % pn.split)

    barrier = pltpu.get_barrier_semaphore()

    def greet(k, carry):
        pl.semaphore_signal(barrier, inc=1, device_id=in_target(unit_of(k)), device_id_type=MESH)
        return carry

    def greet_back(k, carry):
        tgt = out_target(lax.rem(g * pn.split + sub + k, pn.units))
        pl.semaphore_signal(barrier, inc=1, device_id=tgt, device_id_type=MESH)
        return carry

    me_source = g * pn.split + sub
    lax.fori_loop(1, pn.units, greet, 0)
    for k in range(pn.units):
        tgt = out_target(k)

        @pl.when(jnp.logical_or(tgt[0] != g, tgt[1] != p))
        def _(tgt=tgt):
            pl.semaphore_signal(barrier, inc=1, device_id=tgt, device_id_type=MESH)

    @pl.when(jnp.logical_not(home))
    def _():
        pl.semaphore_signal(barrier, inc=1, device_id=in_target(unit), device_id_type=MESH)

    @pl.when(has_left)
    def _():
        pl.semaphore_signal(barrier, inc=1, device_id=(g, p - 1), device_id_type=MESH)

    @pl.when(has_right)
    def _():
        pl.semaphore_signal(barrier, inc=1, device_id=(g, p + 1), device_id_type=MESH)

    expected = (
        2 * pn.units - jnp.where(home, 2, 0)
        + jnp.where(has_left, 1, 0) + jnp.where(has_right, 1, 0)
    )
    pl.semaphore_wait(barrier, expected)

    for mid in range(pn.mids):
        for k in range(1, pn.units):
            u = unit_of(k)
            pltpu.make_async_remote_copy(
                src_ref=x_ref.at[mid, u],
                dst_ref=buf.at[0, mid * pn.genes + g, rows(pn.first + sub * pn.width, pn.width)],
                send_sem=in_send.at[mid, u],
                recv_sem=in_recv.at[mid, me_source],
                device_id=in_target(u),
                device_id_type=MESH,
            ).start()
        own_dst = buf.at[0, mid * pn.genes + g, rows(pn.first + sub * pn.width, pn.width)]

        @pl.when(home)
        def _(mid=mid, own_dst=own_dst):
            pltpu.make_async_copy(x_ref.at[mid, unit], own_dst, in_recv.at[mid, me_source]).start()

        @pl.when(jnp.logical_not(home))
        def _(mid=mid, own_dst=own_dst):
            pltpu.make_async_remote_copy(
                src_ref=x_ref.at[mid, unit],
                dst_ref=own_dst,
                send_sem=in_send.at[mid, unit],
                recv_sem=in_recv.at[mid, me_source],
                device_id=in_target(unit),
                device_id_type=MESH,
            ).start()

    nz = pn.size_z
    full = (pn.layers * ny, nz)
    start_x = r * pn.cells
    cell = lax.broadcasted_iota(jnp.int32, full, 0) // ny - pn.first + start_x
    inside = jnp.logical_and(cell >= 0, cell < pn.total_x)
    coord = (cell.astype(jnp.float32) + 0.5) / pn.total_x
    step_x = 1.0 / pn.total_x
    half = 0.5 * TIME_STEP
    yi = lax.broadcasted_iota(jnp.int32, (ny, nz), 0)
    zi = lax.broadcasted_iota(jnp.int32, (8, nz), 1)
    y_at = (yi.astype(jnp.float32) + 0.5) / ny
    z_at = (zi.astype(jnp.float32) + 0.5) / nz

    zero_side = jnp.zeros((pn.first * ny, nz), jnp.float32)

    from_z = lax.broadcasted_iota(jnp.int32, (2 * nz, 2 * nz), 0) % nz
    to_z = lax.broadcasted_iota(jnp.int32, (2 * nz, 2 * nz), 1)
    wanted = jnp.where(to_z < nz, to_z + 1, to_z - nz - 1)
    shift[...] = jnp.where(from_z == wanted, 1.0, 0.0).astype(shift.dtype)

    def tables(t, carry):
        mid, gene = t // pn.genes, t % pn.genes
        at = gene * (pn.mids * pn.units) + mid * pn.units + unit
        lev = [levels_ref[rate_ref[at * 3 + k]] for k in range(3)]
        tab_u[t] = jnp.where(inside, TIME_STEP * DIFF - half * (lev[0] - (coord + step_x)), 0.0)
        tab_d[t] = jnp.where(inside, TIME_STEP * DIFF + half * (lev[0] - (coord - step_x)), 0.0)
        tab_y[t, 0] = jnp.where(yi < ny - 1, TIME_STEP * DIFF - half * (lev[1] - (y_at + 1.0 / ny)), 0.0)
        tab_y[t, 1] = jnp.where(yi > 0, TIME_STEP * DIFF + half * (lev[1] - (y_at - 1.0 / ny)), 0.0)
        tab_z[t, 0] = jnp.where(zi < nz - 1, TIME_STEP * DIFF - half * (lev[2] - (z_at + 1.0 / nz)), 0.0)
        tab_z[t, 1] = jnp.where(zi > 0, TIME_STEP * DIFF + half * (lev[2] - (z_at - 1.0 / nz)), 0.0)
        for side in range(2):
            buf[side, t, rows(0, pn.first)] = zero_side
            buf[side, t, rows(pn.first + pn.cells, pn.first)] = zero_side
        return carry

    lax.fori_loop(0, TOP, tables, 0)

    own = (pn.cells * ny, nz)
    own_cell = lax.broadcasted_iota(jnp.int32, own, 0) // ny + start_x
    own_x = (own_cell.astype(jnp.float32) + 0.5) / pn.total_x
    hill = 0.1 + own_x * own_x / (0.09 + own_x * own_x)
    for b in range(BLOCKS):
        bit = STATE_BITS - 1 - order_ref[b]
        act = on_ref[bit] * hill
        rate = act + off_ref[bit]
        share = act / rate
        decay = jnp.exp(-rate)
        gone = 1.0 - decay
        up = share * gone
        down = (1.0 - share) * gone
        tab_s[b, 0, 0] = 1.0 - up
        tab_s[b, 0, 1] = down
        tab_s[b, 1, 0] = 1.0 - down
        tab_s[b, 1, 1] = up

    def wait_in(mid):
        def one(k, carry):
            gs, js = k // pn.split, k % pn.split
            dst = buf.at[0, mid * pn.genes + gs, rows(pn.first + js * pn.width, pn.width)]
            pltpu.make_async_copy(x_ref.at[0, 0], dst, in_recv.at[mid, k]).wait()
            return carry

        lax.fori_loop(0, pn.units, one, 0)

    groups = TOP // GROUP

    def edge_copies(side, gr):
        states = pl.ds(gr * GROUP, GROUP)
        right = pltpu.make_async_remote_copy(
            src_ref=buf.at[side, states, rows(pn.first + pn.cells - pn.halo, pn.halo)],
            dst_ref=land.at[side, 0, states],
            send_sem=halo_send.at[side, 0, gr],
            recv_sem=halo_recv.at[side, 0, gr],
            device_id=(g, p + 1),
            device_id_type=MESH,
        )
        left = pltpu.make_async_remote_copy(
            src_ref=buf.at[side, states, rows(pn.first, pn.halo)],
            dst_ref=land.at[side, 1, states],
            send_sem=halo_send.at[side, 1, gr],
            recv_sem=halo_recv.at[side, 1, gr],
            device_id=(g, p - 1),
            device_id_type=MESH,
        )
        return left, right

    def send_edges(side, gr):
        left, right = edge_copies(side, gr)
        pl.when(has_left)(left.start)
        pl.when(has_right)(right.start)

    def take_edges(side, gr):
        left, right = edge_copies(side, gr)

        @pl.when(has_left)
        def _():
            right.wait_recv()
            left.wait_send()

        @pl.when(has_right)
        def _():
            left.wait_recv()
            right.wait_send()

        def place(i, carry):
            t = gr * GROUP + i

            @pl.when(has_left)
            def _():
                buf[side, t, rows(pn.first - pn.halo, pn.halo)] = land[side, 0, t]

            @pl.when(has_right)
            def _():
                buf[side, t, rows(pn.first + pn.cells, pn.halo)] = land[side, 1, t]

            return carry

        lax.fori_loop(0, GROUP, place, 0)

    def update(src, dst, t, start, n, cy, cz, z_row):
        at = start * ny
        size = n * ny

        def read(off):
            return buf[src, t, pl.ds(at + off, size)]

        here = read(0)
        shape3 = (n, ny, nz)
        out = 0.1 * here if DIFF == 1.0 else (1.0 - 6.0 * TIME_STEP * DIFF) * here
        out = out + tab_u[t, pl.ds(at, size)] * read(ny) + tab_d[t, pl.ds(at, size)] * read(-ny)
        along_y = cy[0][None] * read(1).reshape(shape3) + cy[1][None] * read(-1).reshape(shape3)
        z_next = pair[pl.ds(z_row, size), :nz].reshape(n * ny // 8, 8, nz)
        z_last = pair[pl.ds(z_row, size), nz:].reshape(n * ny // 8, 8, nz)
        along_z = cz[0][None] * z_next + cz[1][None] * z_last
        buf[dst, t, pl.ds(at, size)] = out + along_y.reshape(size, nz) + along_z.reshape(size, nz)

    sides = min(pn.slabs - 1, 2)

    def diffuse(side, gr):
        src, dst = side, 1 - side
        for i in range(SUBSTEPS):
            extra = SUBSTEPS - 1 - i
            if sides == 0:
                begin, n = pn.first, pn.cells
            elif sides == 1:
                begin, n = pn.first - jnp.where(has_left, extra, 0), pn.cells + extra
            else:
                begin, n = pn.first - extra, pn.cells + 2 * extra
            size = n * ny
            here = buf[src, pl.ds(gr * GROUP, GROUP), rows(begin, n)].reshape(GROUP * size, nz)
            high = here.astype(jnp.bfloat16)
            low = (here - high.astype(jnp.float32)).astype(jnp.bfloat16)
            pair[pl.ds(0, GROUP * size)] = jnp.dot(
                jnp.concatenate([high, low], axis=1), shift[...], preferred_element_type=jnp.float32
            )

            def one(j, carry, src=src, dst=dst, begin=begin, n=n, size=size):
                t = gr * GROUP + j
                cy = (tab_y[t, 0], tab_y[t, 1])
                cz = (tab_z[t, 0], tab_z[t, 1])
                pieces = -(-n // CHUNK)
                done = 0
                for c in range(pieces):
                    take = (n - done) // (pieces - c)
                    z_row = pl.multiple_of(j * size + done * ny, ny)
                    update(src, dst, t, begin + done, take, cy, cz, z_row)
                    done += take
                return carry

            lax.fori_loop(0, GROUP, one, 0)
            src, dst = dst, src

    own_rows = rows(pn.first, pn.cells)

    def switch(b, side, t):
        order = order_ref[b]
        mask = jnp.int32(pn.masks[BLOCKS - 1])
        for k in range(BLOCKS - 1):
            mask = jnp.where(order == k, jnp.int32(pn.masks[k]), mask)
        mate = t ^ mask
        high = jnp.where((t & mask) != 0, 1, 0)
        buf[1 - side, t, own_rows] = (
            tab_s[b, high, 0] * buf[side, t, own_rows] + tab_s[b, high, 1] * buf[side, mate, own_rows]
        )

    fin = BLOCKS % 2

    def out_src(mid, u):
        return buf.at[
            fin, mid * pn.genes + u // pn.split, rows(pn.first + (u % pn.split) * pn.width, pn.width)
        ]

    def send_out(mid):
        for k in range(pn.units):
            u = lax.rem(unit + k, pn.units)
            tgt = out_target(u)
            mine = jnp.logical_and(tgt[0] == g, tgt[1] == p)

            @pl.when(mine)
            def _(mid=mid, u=u):
                pltpu.make_async_copy(out_src(mid, u), out_ref.at[mid, unit], out_recv.at[mid, unit]).start()

            @pl.when(jnp.logical_not(mine))
            def _(mid=mid, u=u, tgt=tgt):
                pltpu.make_async_remote_copy(
                    src_ref=out_src(mid, u),
                    dst_ref=out_ref.at[mid, unit],
                    send_sem=out_send.at[mid, u],
                    recv_sem=out_recv.at[mid, unit],
                    device_id=tgt,
                    device_id_type=MESH,
                ).start()

    stepwise = pn.genes == GROUP
    if not stepwise:
        for mid in range(pn.mids):
            wait_in(mid)

    def first_block(gr, carry):
        @pl.when(gr < groups)
        def _():
            if stepwise:
                wait_in(gr)
            send_edges(0, gr)

        @pl.when(gr > 0)
        def _():
            take_edges(0, gr - 1)
            diffuse(0, gr - 1)

        return carry

    lax.fori_loop(0, groups + 1, first_block, 0)

    def next_block(b, carry):
        side = lax.rem(b, 2)
        after = 1 - side

        def flip(gr, c):
            lax.fori_loop(0, GROUP, lambda i, k: (switch(b, side, gr * GROUP + i), k)[1], 0)
            send_edges(after, gr)
            return c

        def spread(gr, c):
            take_edges(after, gr)
            diffuse(after, gr)
            return c

        lax.fori_loop(0, groups, flip, 0)
        lax.fori_loop(0, groups, spread, 0)
        return carry

    lax.fori_loop(0, BLOCKS - 1, next_block, 0)

    for gr in range(groups):
        lax.fori_loop(
            0, GROUP,
            lambda i, k, gr=gr: (switch(BLOCKS - 1, (BLOCKS - 1) % 2, gr * GROUP + i), k)[1], 0,
        )
        if stepwise:
            send_out(gr)
    if not stepwise:
        for mid in range(pn.mids):
            send_out(mid)

    def finish(k, carry):
        tgt = out_target(k)
        for mid in range(pn.mids):
            pltpu.make_async_copy(out_src(mid, 0), out_ref.at[mid, k], out_recv.at[mid, k]).wait()

            @pl.when(jnp.logical_or(tgt[0] != g, tgt[1] != p))
            def _(mid=mid):
                pltpu.make_async_copy(out_src(mid, k), out_ref.at[mid, 0], out_send.at[mid, k]).wait()

            @pl.when(jnp.logical_or(k != unit, jnp.logical_not(home)))
            def _(mid=mid):
                pltpu.make_async_copy(x_ref.at[mid, k], out_src(mid, 0), in_send.at[mid, k]).wait()

        return carry

    lax.fori_loop(0, pn.units, finish, 0)


def local(density, levels, rate_index, on_rate, off_rate, gene_order):
    count, width_x, size_y, size_z = density.shape
    pn = Plan(lax.axis_size("gene"), lax.axis_size("prot"), count, width_x, size_y, size_z)
    rates = lax.all_gather(rate_index.reshape(-1), "gene", tiled=True)
    shape = (pn.mids, pn.units, width_x * size_y, size_z)
    smem = pl.BlockSpec(memory_space=pltpu.SMEM)
    hbm = pl.BlockSpec(memory_space=pl.ANY)
    f32 = jnp.float32
    vec = (pn.layers * size_y, size_z)
    out = pl.pallas_call(
        partial(body, pn),
        out_shape=jax.ShapeDtypeStruct(shape, f32),
        in_specs=[hbm] + [smem] * 5,
        out_specs=hbm,
        scratch_shapes=[
            pltpu.VMEM((2, TOP) + vec, f32),
            pltpu.VMEM((2, 2, TOP, pn.halo * size_y, size_z), f32),
            pltpu.VMEM((TOP,) + vec, f32),
            pltpu.VMEM((TOP,) + vec, f32),
            pltpu.VMEM((TOP, 2, size_y, size_z), f32),
            pltpu.VMEM((TOP, 2, 8, size_z), f32),
            pltpu.VMEM((BLOCKS, 2, 2, pn.cells * size_y, size_z), f32),
            pltpu.VMEM((2 * size_z, 2 * size_z), jnp.bfloat16),
            pltpu.VMEM((GROUP * vec[0], 2 * size_z), f32),
            pltpu.SemaphoreType.DMA((pn.mids, pn.units)),
            pltpu.SemaphoreType.DMA((pn.mids, pn.units)),
            pltpu.SemaphoreType.DMA((pn.mids, pn.units)),
            pltpu.SemaphoreType.DMA((pn.mids, pn.units)),
            pltpu.SemaphoreType.DMA((2, 2, TOP // GROUP)),
            pltpu.SemaphoreType.DMA((2, 2, TOP // GROUP)),
        ],
        compiler_params=pltpu.CompilerParams(
            collective_id=0, has_side_effects=True, vmem_limit_bytes=60 * 1024 * 1024
        ),
        name="exchange_evolve",
    )(density.reshape(shape), rates, levels, on_rate, off_rate, gene_order)
    return out.reshape(density.shape)


def solution(mesh):
    in_specs = (P("gene", "prot", None, None), P(), P("gene", None), P(), P(), P())
    out_specs = P("gene", "prot", None, None)
    return jax.shard_map(local, mesh=mesh, in_specs=in_specs, out_specs=out_specs, check_vma=False)
```

profile of v0, /device:TPU:9, one launch (start us, length us, event | category | flops | bytes accessed | tf_op | source)
XLA Modules:
  0.0 254.1 jit_solution(8127109045683051638)
XLA Ops:
  0.0 1.2 dynamic-slice
  1.9 0.8 copy.7
  2.7 0.1 reshape.12
  2.8 0.2 dynamic-update-slice
  3.1 5.9 %all-reduce.rate_ref = s32[768]{0:T(1024)} all-reduce(s32[768]{0:T(1024)S(1)} %dynamic-update-slice), channel_id=1, replica_groups=mesh['gene'=4,'prot'=8] {'gene'}, use_global_device_ids=true, to_apply=%add | all-reduce | flops 768 | bytes 6144
  9.0 241.3 %exchange_evolve.1 = f32[4,16,96,128]{3,2,1,0:T(8,128)} custom-call(f32[4,16,96,128]{3,2,1,0:T(8,128)} %bitcast.4, s32[768]{0:T(1024)} %all-reduce.rate_ref, f32[8]{0:T(128)} %levels_ref.1, f32[8]{0:T(128)} %on_ref.1, f32[8]{0:T(128)} %off_ref.1, s32[4]{0:T(128)} %order_ref.1), custom_call_target="tpu_custom_call" | custom-call | tf_op jit(solution)/shard_map/exchange_evolve/pallas_call | solution.py:429
  250.3 3.8 %copy.10 = f32[64,6,16,128]{3,2,1,0:T(8,128)} copy(f32[64,6,16,128]{3,2,1,0:T(8,128)} %bitcast.3) | data formatting | bytes 6291456
  (1 shorter events, 0.0 us)
where the time goes:
time: 256 us; the launch traced here: 254 us
  Pallas kernels  241 us (94%)
  local copies, waits for them, and re-layouts  6.16 us (2%)
  blocking collectives  5.94 us (2%)
    pallas_call x1, Pallas kernels, local(): pl.pallas_call(partial(body, pn), out_shape=jax.ShapeDtypeStruct(shape, f...  241 us
    unnamed x5, local copies, waits for them, and re-layouts  6.02 us
    unnamed x1, blocking collectives  5.94 us

commit v1 on v0

v1 whole, which is shorter than its diff:
```python
from functools import partial

import jax
import jax.numpy as jnp
from jax import lax
from jax.experimental import pallas as pl
from jax.experimental.pallas import tpu as pltpu
from jax.sharding import PartitionSpec as P

STATE_BITS = 8
BLOCKS = 4
SUBSTEPS = 6
DIFF = 1.0
TIME_STEP = 0.15
KEEP = 1.0 - 6.0 * TIME_STEP * DIFF
TOP = 2**BLOCKS
PIECE = 16
MESH = pl.DeviceIdType.MESH


class Plan:
    def __init__(self, genes, prots, count, width, size_y, size_z):
        self.genes, self.prots = genes, prots
        self.units = count * genes // TOP
        self.mids = count // self.units
        self.slots = self.units // genes
        self.width, self.size_y, self.size_z = width, size_y, size_z
        self.total_x = width * prots
        self.halo = SUBSTEPS
        self.layers = width + 2 * self.halo
        assert self.slots * genes == self.units and self.mids * genes == TOP
        assert width >= self.halo


def body(
    pn, x_ref, rate_ref, levels_ref, on_ref, off_ref, order_ref, out_ref,
    near, post, work, rates, tab_x, tab_y, tab_z, tab_s,
    own_sem, halo_send, halo_recv, move_send, move_recv, out_send, out_recv, rate_send, rate_recv,
):
    g, p = lax.axis_index("gene"), lax.axis_index("prot")
    ny, nz = pn.size_y, pn.size_z
    genes, mids, slots, halo, width = pn.genes, pn.mids, pn.slots, pn.halo, pn.width
    has_left, has_right = p > 0, p < pn.prots - 1

    def rows(layer, n):
        return pl.ds(layer * ny, n * ny)

    def flip(a, d):
        out, bit = 0, 1
        while bit < genes:
            i, j = lax.rem(lax.div(a, bit), 2), lax.rem(lax.div(d, bit), 2)
            out = out + (i + j - 2 * i * j) * bit
            bit *= 2
        return out

    def order_of(j):
        return flip(g, genes - 1 - j)

    own, left_rows, right_rows = rows(halo, width), rows(0, halo), rows(halo + width, halo)

    barrier = pltpu.get_barrier_semaphore()

    def greet(d, carry):
        pl.semaphore_signal(barrier, inc=1, device_id=(flip(g, d), p), device_id_type=MESH)
        return carry

    lax.fori_loop(1, genes, greet, 0)

    @pl.when(has_left)
    def _():
        pl.semaphore_signal(barrier, inc=1, device_id=(g, p - 1), device_id_type=MESH)

    @pl.when(has_right)
    def _():
        pl.semaphore_signal(barrier, inc=1, device_id=(g, p + 1), device_id_type=MESH)

    pl.semaphore_wait(barrier, genes - 1 + jnp.where(has_left, 1, 0) + jnp.where(has_right, 1, 0))

    def edges(par, k, grp, from_input):
        def side(first, dst_rows, way, to):
            if from_input:
                src = x_ref.at[:, grp * slots + k, rows(first, halo)]
            else:
                src = near.at[par, k, grp, :, rows(halo + first, halo)]
            return pltpu.make_async_remote_copy(
                src_ref=src,
                dst_ref=near.at[par, k, grp, :, dst_rows],
                send_sem=halo_send.at[par, way, k, grp],
                recv_sem=halo_recv.at[par, way, k, grp],
                device_id=(g, to),
                device_id_type=MESH,
            )

        return side(width - halo, left_rows, 0, p + 1), side(0, right_rows, 1, p - 1)

    def send_edges(par, k, grp, from_input):
        to_right, to_left = edges(par, k, grp, from_input)
        pl.when(has_right)(to_right.start)
        pl.when(has_left)(to_left.start)

    def sent_edges(par, k, grp):
        to_right, to_left = edges(par, k, grp, False)
        pl.when(has_right)(to_right.wait_send)
        pl.when(has_left)(to_left.wait_send)

    def take_edges(par, k, grp):
        to_right, to_left = edges(par, k, grp, False)
        pl.when(has_left)(to_right.wait_recv)
        pl.when(has_right)(to_left.wait_recv)

    def own_copy(k, grp):
        return pltpu.make_async_copy(
            x_ref.at[:, grp * slots + k], near.at[0, k, grp, :, own], own_sem.at[k, grp]
        )

    def open_sub(i, carry):
        k, grp = lax.div(i, genes), order_of(lax.rem(i, genes))
        send_edges(0, k, grp, True)
        own_copy(k, grp).start()
        return carry

    lax.fori_loop(0, slots * genes, open_sub, 0)

    def rate_copy(to):
        return pltpu.make_async_remote_copy(
            src_ref=rate_ref,
            dst_ref=rates.at[g],
            send_sem=rate_send.at[to],
            recv_sem=rate_recv.at[g],
            device_id=(to, p),
            device_id_type=MESH,
        )

    def send_rates(d, carry):
        rate_copy(flip(g, d)).start()
        return carry

    lax.fori_loop(1, genes, send_rates, 0)

    cell = lax.broadcasted_iota(jnp.int32, (pn.layers * ny, nz), 0) // ny - halo + p * width
    inside = jnp.logical_and(cell >= 0, cell < pn.total_x)
    coord = (cell.astype(jnp.float32) + 0.5) / pn.total_x
    step_x = 1.0 / pn.total_x
    base, half = TIME_STEP * DIFF / KEEP, 0.5 * TIME_STEP / KEEP
    yi = lax.broadcasted_iota(jnp.int32, (ny, nz), 0)
    zi = lax.broadcasted_iota(jnp.int32, (8, nz), 1)
    y_at = (yi.astype(jnp.float32) + 0.5) / ny
    z_at = (zi.astype(jnp.float32) + 0.5) / nz

    def tables(l, carry):
        lev = levels_ref[l]
        tab_x[l, 0] = jnp.where(inside, base - half * (lev - (coord + step_x)), 0.0)
        tab_x[l, 1] = jnp.where(inside, base + half * (lev - (coord - step_x)), 0.0)
        tab_y[l, 0] = jnp.where(yi < ny - 1, base - half * (lev - (y_at + 1.0 / ny)), 0.0)
        tab_y[l, 1] = jnp.where(yi > 0, base + half * (lev - (y_at - 1.0 / ny)), 0.0)
        tab_z[l, 0] = jnp.where(zi < nz - 1, base - half * (lev - (z_at + 1.0 / nz)), 0.0)
        tab_z[l, 1] = jnp.where(zi > 0, base + half * (lev - (z_at - 1.0 / nz)), 0.0)
        return carry

    lax.fori_loop(0, levels_ref.shape[0], tables, 0)

    def blank(i, carry):
        par, k, grp = lax.div(i, slots * genes), lax.rem(lax.div(i, genes), slots), lax.rem(i, genes)
        zero = jnp.zeros((mids, halo * ny, nz), jnp.float32)

        @pl.when(jnp.logical_not(has_left))
        def _():
            near[par, k, grp, :, left_rows] = zero

        @pl.when(jnp.logical_not(has_right))
        def _():
            near[par, k, grp, :, right_rows] = zero

        return carry

    lax.fori_loop(0, 2 * slots * genes, blank, 0)

    scale = KEEP**SUBSTEPS
    own_cell = lax.broadcasted_iota(jnp.int32, (width, 8, nz), 0) + p * width
    own_x = (own_cell.astype(jnp.float32) + 0.5) / pn.total_x
    hill = 0.1 + own_x * own_x / (0.09 + own_x * own_x)
    for b in range(BLOCKS):
        bit = STATE_BITS - 1 - order_ref[b]
        act = on_ref[bit] * hill
        rate = act + off_ref[bit]
        share = act / rate
        gone = 1.0 - jnp.exp(-rate)
        up = share * gone
        down = (1.0 - share) * gone
        tab_s[b, 0, 0] = (1.0 - up) * scale
        tab_s[b, 0, 1] = down * scale
        tab_s[b, 1, 0] = (1.0 - down) * scale
        tab_s[b, 1, 1] = up * scale

    def own_rates(s, carry):
        for k in range(3):
            rates[g, k, s] = rate_ref[k, s]
        return carry

    lax.fori_loop(0, rate_ref.shape[1], own_rates, 0)

    def spread(src, start, n, c):
        at, size = start * ny, n * ny

        def read(off):
            return src[pl.ds(at + off, size)]

        here = read(0)
        out = here + c[0][pl.ds(at, size)] * read(ny) + c[1][pl.ds(at, size)] * read(-ny)
        by_y, by_z = (n, ny, nz), (size // 8, 8, nz)
        along_y = c[2][None] * read(1).reshape(by_y) + c[3][None] * read(-1).reshape(by_y)
        z_next = pltpu.roll(here, nz - 1, axis=1).reshape(by_z)
        z_last = pltpu.roll(here, 1, axis=1).reshape(by_z)
        along_z = c[4][None] * z_next + c[5][None] * z_last
        return out + along_y.reshape(size, nz) + along_z.reshape(size, nz)

    def diffuse(b, k, grp):
        first = b == 0
        who = jnp.where(first, g, grp)
        unit = jnp.where(first, grp * slots + k, g * slots + k)
        par, to = lax.rem(b, 2), jnp.minimum(b, 1)
        coef = []
        for m in range(mids):
            lev = [rates[who, d, m * pn.units + unit] for d in range(3)]
            coef.append(
                (
                    tab_x.at[lev[0], 0], tab_x.at[lev[0], 1], tab_y[lev[1], 0], tab_y[lev[1], 1],
                    tab_z[lev[2], 0], tab_z[lev[2], 1],
                )
            )
        for i in range(SUBSTEPS):
            extra = SUBSTEPS - 1 - i
            start, stop = halo - extra, halo + width + extra
            for at in range(start, stop, PIECE):
                n = min(PIECE, stop - at)
                for m in range(mids):
                    src = near.at[par, k, grp, m] if i == 0 else work.at[(i + 1) % 2, m]
                    new = spread(src, at, n, coef[m])
                    if i < SUBSTEPS - 1:
                        work[i % 2, m, rows(at, n)] = new
                    else:
                        post[to, k, grp, m, rows(at - halo, n)] = new

    def move(k, grp):
        return pltpu.make_async_remote_copy(
            src_ref=post.at[0, k, grp],
            dst_ref=post.at[1, k, g],
            send_sem=move_send.at[k, grp],
            recv_sem=move_recv.at[k, g],
            device_id=(grp, p),
            device_id_type=MESH,
        )

    def local_wait(k, grp, sem):
        pltpu.make_async_copy(post.at[0, k, grp], post.at[1, k, grp], sem).wait()

    def sub(b, k, j):
        grp = order_of(j)
        take_edges(lax.rem(b, 2), k, grp)
        first, last = b == 0, j == genes - 1

        @pl.when(first)
        def _():
            own_copy(k, grp).wait()

        diffuse(b, k, grp)

        @pl.when(jnp.logical_and(first, jnp.logical_not(last)))
        def _():
            move(k, grp).start()

        @pl.when(jnp.logical_and(first, last))
        def _():
            post[1, k, g] = post[0, k, g]

    def out_copy(k, grp):
        return pltpu.make_async_remote_copy(
            src_ref=near.at[BLOCKS % 2, k, grp, :, own],
            dst_ref=out_ref.at[:, g * slots + k],
            send_sem=out_send.at[k, grp],
            recv_sem=out_recv.at[k, g],
            device_id=(grp, p),
            device_id_type=MESH,
        )

    def keep_copy(k):
        return pltpu.make_async_copy(
            near.at[BLOCKS % 2, k, g, :, own], out_ref.at[:, g * slots + k], out_recv.at[k, g]
        )

    def switch(i, carry):
        b, k = lax.div(i, slots), lax.rem(i, slots)
        par = lax.rem(b + 1, 2)

        @pl.when(b == 0)
        def _():
            def arrived(d, c):
                grp = flip(g, d)
                local_wait(k, grp, move_recv.at[k, grp])
                return c

            lax.fori_loop(1, genes, arrived, 0)

        @pl.when(b > 0)
        def _():
            lax.fori_loop(0, genes, lambda grp, c: (sent_edges(par, k, grp), c)[1], 0)

        order = order_ref[b]
        picks = [order == q for q in range(BLOCKS)]
        masks = [TOP >> (q + 1) for q in range(BLOCKS)]

        def of_mask(values):
            out = values[-1]
            for q in range(BLOCKS - 1):
                out = lax.select(picks[q], values[q], out)
            return out

        high = [of_mask([jnp.int32(1 if t & mask else 0) for mask in masks]) for t in range(TOP)]

        def strip(r, c):
            layer = lax.div(r * 8, ny)
            at = pl.ds(pl.multiple_of(r * 8, 8), 8)
            to = pl.ds(pl.multiple_of(halo * ny + r * 8, 8), 8)
            held = [post[1, k, t // mids, t % mids, at] for t in range(TOP)]
            for t in range(TOP):
                mate = of_mask([held[t ^ mask] for mask in masks])
                near[par, k, t // mids, t % mids, to] = (
                    tab_s[b, high[t], 0, layer] * held[t] + tab_s[b, high[t], 1, layer] * mate
                )
            return c

        lax.fori_loop(0, width * ny // 8, strip, 0)

        @pl.when(b < BLOCKS - 1)
        def _():
            lax.fori_loop(0, genes, lambda j, c: (send_edges(par, k, order_of(j), False), c)[1], 0)

        @pl.when(b == BLOCKS - 1)
        def _():
            lax.fori_loop(0, genes - 1, lambda j, c: (out_copy(k, order_of(j)).start(), c)[1], 0)
            keep_copy(k).start()

        return carry

    def step(i, carry):
        b, k = lax.div(i, slots), lax.rem(i, slots)
        lax.fori_loop(0, genes, lambda j, c: (sub(b, k, j), c)[1], 0)

        @pl.when(i == slots - 1)
        def _():
            def arrived(d, c):
                grp = flip(g, d)
                pltpu.make_async_copy(rates.at[grp], rates.at[grp], rate_recv.at[grp]).wait()
                return c

            lax.fori_loop(1, genes, arrived, 0)

        first, last = b == 0, k == slots - 1
        begin = jnp.where(first, jnp.maximum(k - 1, 0), i)
        end = jnp.where(first, jnp.where(last, k + 1, k), i + 1)
        lax.fori_loop(begin, end, switch, 0)
        return carry

    lax.fori_loop(0, BLOCKS * slots, step, 0)

    def finish(i, carry):
        k, grp = lax.div(i, genes), lax.rem(i, genes)
        sent_edges(1 - BLOCKS % 2, k, grp)

        @pl.when(grp != g)
        def _():
            local_wait(k, grp, move_send.at[k, grp])
            out_copy(k, grp).wait_send()

        pltpu.make_async_copy(
            near.at[BLOCKS % 2, k, grp, :, own], out_ref.at[:, grp * slots + k], out_recv.at[k, grp]
        ).wait()
        return carry

    lax.fori_loop(0, slots * genes, finish, 0)
    lax.fori_loop(1, genes, lambda d, c: (rate_copy(flip(g, d)).wait_send(), c)[1], 0)


def local(density, levels, rate_index, on_rate, off_rate, gene_order):
    count, width_x, size_y, size_z = density.shape
    pn = Plan(lax.axis_size("gene"), lax.axis_size("prot"), count, width_x, size_y, size_z)
    shape = (pn.mids, pn.units, width_x * size_y, size_z)
    smem = pl.BlockSpec(memory_space=pltpu.SMEM)
    hbm = pl.BlockSpec(memory_space=pl.ANY)
    f32 = jnp.float32
    tall = (pn.layers * size_y, size_z)
    per_sub = (pn.slots, pn.genes)
    dma = pltpu.SemaphoreType.DMA
    out = pl.pallas_call(
        partial(body, pn),
        out_shape=jax.ShapeDtypeStruct(shape, f32),
        in_specs=[hbm] + [smem] * 5,
        out_specs=hbm,
        scratch_shapes=[
            pltpu.VMEM((2,) + per_sub + (pn.mids,) + tall, f32),
            pltpu.VMEM((2,) + per_sub + (pn.mids, width_x * size_y, size_z), f32),
            pltpu.VMEM((2, pn.mids) + tall, f32),
            pltpu.SMEM((pn.genes, 3, count), jnp.int32),
            pltpu.VMEM(levels.shape + (2,) + tall, f32),
            pltpu.VMEM(levels.shape + (2, size_y, size_z), f32),
            pltpu.VMEM(levels.shape + (2, 8, size_z), f32),
            pltpu.VMEM((BLOCKS, 2, 2, width_x, 8, size_z), f32),
            dma(per_sub),
            dma((2, 2) + per_sub),
            dma((2, 2) + per_sub),
            dma(per_sub),
            dma(per_sub),
            dma(per_sub),
            dma(per_sub),
            dma((pn.genes,)),
            dma((pn.genes,)),
        ],
        compiler_params=pltpu.CompilerParams(
            collective_id=0, has_side_effects=True, vmem_limit_bytes=60 * 1024 * 1024
        ),
        name="exchange_evolve",
    )(density.reshape(shape), rate_index.T, levels, on_rate, off_rate, gene_order)
    return out.reshape(density.shape)


def solution(mesh):
    in_specs = (P("gene", "prot", None, None), P(), P("gene", None), P(), P(), P())
    out_specs = P("gene", "prot", None, None)
    return jax.shard_map(local, mesh=mesh, in_specs=in_specs, out_specs=out_specs, check_vma=False)
```

time: 256 us -> 158 us (0.62)
  Pallas kernels: 241 us -> 154 us
  blocking collectives: 5.94 us -> 0 us
    pallas_call x1, Pallas kernels: 241 us -> 154 us  [local(): pl.pallas_call(partial(body, pn), out_shape=jax.ShapeDtypeStruct(shape, f...]
    unnamed x1 -> x0, blocking collectives: 5.94 us -> none
    unnamed x5 -> x1, local copies, waits for them, and re-layouts: 6.02 us -> 3.76 us
where the time goes in v1:
time: 158 us
  Pallas kernels  154 us (97%)
  local copies, waits for them, and re-layouts  3.76 us (2%)
    pallas_call x1, Pallas kernels, local(): pl.pallas_call(partial(body, pn), out_shape=jax.ShapeDtypeStruct(shape, f...  154 us
    unnamed x1, local copies, waits for them, and re-layouts  3.76 us

profile of v1, /device:TPU:9, one launch (start us, length us, event | category | flops | bytes accessed | tf_op | source)
XLA Modules:
  0.0 157.9 jit_solution(6175546930801110588)
XLA Ops:
  0.0 154.2 %exchange_evolve.1 = f32[4,16,96,128]{3,2,1,0:T(8,128)} custom-call(f32[4,16,96,128]{3,2,1,0:T(8,128)} %bitcast.4, s32[3,64]{1,0:T(4,128)} %bitcast.5, f32[8]{0:T(128)} %levels_ref.1, f32[8]{0:T(128)} %on_ref.1, f32[8]{0:T(128)} %off_ref.1, s32[4]{0:T(128)} %order_ref.1), custom_call_target="tpu_custom_call" | custom-call | tf_op jit(solution)/shard_map/exchange_evolve/pallas_call | solution.py:394
  154.2 3.8 %copy.8 = f32[64,6,16,128]{3,2,1,0:T(8,128)} copy(f32[64,6,16,128]{3,2,1,0:T(8,128)} %bitcast.3) | data formatting | bytes 6291456

commit v2 on v1

v2 whole, which is shorter than its diff:
```python
from functools import partial

import jax
import jax.numpy as jnp
from jax import lax
from jax.experimental import pallas as pl
from jax.experimental.pallas import tpu as pltpu
from jax.sharding import PartitionSpec as P

STATE_BITS = 8
BLOCKS = 4
SUBSTEPS = 6
DIFF = 1.0
TIME_STEP = 0.15
KEEP = 1.0 - 6.0 * TIME_STEP * DIFF
TOP = 2**BLOCKS
BATCH = 2
PIECE = 16
ORDER = (12, 8, 4, 13, 14, 9, 5, 15, 10, 6, 11, 7, 0, 1, 2, 3)
MASKS = tuple(TOP >> (q + 1) for q in range(BLOCKS))
MESH = pl.DeviceIdType.MESH


def final_after():
    batch_of = {r: s // BATCH for s, r in enumerate(ORDER)}
    last = {r: max(batch_of[a] for a in [r] + [r ^ mask for mask in MASKS]) for r in range(TOP)}
    return [[r for r in ORDER if last[r] == i] for i in range(TOP // BATCH)]


class Plan:
    def __init__(self, genes, prots, count, width, size_y, size_z):
        self.genes, self.prots = genes, prots
        self.units = count * genes // TOP
        self.mids = count // self.units
        self.slots = self.units // genes
        self.width, self.size_y, self.size_z = width, size_y, size_z
        self.total_x = width * prots
        self.halo = SUBSTEPS
        self.layers = width + 2 * self.halo
        assert self.slots * genes == self.units and self.mids * genes == TOP
        assert width >= self.halo


def body(
    pn, x_ref, rate_ref, levels_ref, on_ref, off_ref, order_ref, out_ref,
    near, post, work, tab_x, tab_y, tab_z, tab_s, rates, levels, on, off, gene_order, lev_tab,
    small_sem, own_sem, halo_send, halo_recv, move_send, move_recv, out_send, out_recv, rate_send, rate_recv,
):
    g, p = lax.axis_index("gene"), lax.axis_index("prot")
    ny, nz = pn.size_y, pn.size_z
    genes, mids, slots, halo, width = pn.genes, pn.mids, pn.slots, pn.halo, pn.width
    has_left, has_right = p > 0, p < pn.prots - 1
    batches = TOP // BATCH
    away = (genes - 1) * mids

    def rows(layer, n):
        return pl.ds(layer * ny, n * ny)

    def flip(a, d):
        out, bit = 0, 1
        while bit < genes:
            i, j = lax.rem(lax.div(a, bit), 2), lax.rem(lax.div(d, bit), 2)
            out = out + (i + j - 2 * i * j) * bit
            bit *= 2
        return out

    peers = [g] + [flip(g, d) for d in range(1, genes)]
    own, left_rows, right_rows = rows(halo, width), rows(0, halo), rows(halo + width, halo)

    small = [
        pltpu.make_async_copy(src, dst, small_sem.at[i])
        for i, (src, dst) in enumerate(
            [
                (rate_ref, rates.at[g]), (levels_ref, levels), (on_ref, on), (off_ref, off),
                (order_ref, gene_order),
            ]
        )
    ]
    for copy in small:
        copy.start()

    barrier = pltpu.get_barrier_semaphore()
    for d in range(1, genes):
        pl.semaphore_signal(barrier, inc=1, device_id=(peers[d], p), device_id_type=MESH)

    @pl.when(has_left)
    def _():
        pl.semaphore_signal(barrier, inc=1, device_id=(g, p - 1), device_id_type=MESH)

    @pl.when(has_right)
    def _():
        pl.semaphore_signal(barrier, inc=1, device_id=(g, p + 1), device_id_type=MESH)

    pl.semaphore_wait(barrier, genes - 1 + jnp.where(has_left, 1, 0) + jnp.where(has_right, 1, 0))

    def edge(src, par, way, k, batch, where):
        return pltpu.make_async_remote_copy(
            src_ref=src,
            dst_ref=near.at[par, k, where, right_rows if way else left_rows],
            send_sem=halo_send.at[par, way, k],
            recv_sem=halo_recv.at[par, way, k, batch],
            device_id=(g, p - 1 if way else p + 1),
            device_id_type=MESH,
        )

    first_layer = (width - halo, 0)
    can_send, can_take = (has_right, has_left), (has_left, has_right)

    def send_edges(par, k, batch):
        where = pl.ds(batch * BATCH, BATCH)
        for way in range(2):
            src = near.at[par, k, where, rows(halo + first_layer[way], halo)]
            pl.when(can_send[way])(edge(src, par, way, k, batch, where).start)

    def sent_edges(par, k):
        for way in range(2):
            src = near.at[par, k, :, left_rows]
            pl.when(can_send[way])(pltpu.make_async_copy(src, src, halo_send.at[par, way, k]).wait)

    def take_edges(par, k, batch):
        for way in range(2):
            dst = near.at[par, k, pl.ds(batch * BATCH, BATCH), right_rows if way else left_rows]
            pl.when(can_take[way])(pltpu.make_async_copy(dst, dst, halo_recv.at[par, way, k, batch]).wait)

    def own_copy(k, s):
        unit = peers[ORDER[s] // mids] * slots + k
        return pltpu.make_async_copy(
            x_ref.at[ORDER[s] % mids, unit], near.at[0, k, s, own], own_sem.at[k, s // BATCH]
        )

    def open_slot(k, carry):
        for way in range(2):

            @pl.when(can_send[way])
            def _(way=way):
                for s, r in enumerate(ORDER):
                    unit = peers[r // mids] * slots + k
                    src = x_ref.at[r % mids, unit, rows(first_layer[way], halo)]
                    edge(src, 0, way, k, s // BATCH, s).start()

        for s in range(TOP):
            own_copy(k, s).start()
        return carry

    lax.fori_loop(0, slots, open_slot, 0)
    for copy in small:
        copy.wait()

    def rate_copy(d):
        return pltpu.make_async_remote_copy(
            src_ref=rates.at[g],
            dst_ref=rates.at[g],
            send_sem=rate_send.at[d],
            recv_sem=rate_recv.at[d],
            device_id=(peers[d], p),
            device_id_type=MESH,
        )

    for d in range(1, genes):
        rate_copy(d).start()

    def look_up(late, k):
        for s, r in enumerate(ORDER):
            who, unit = (peers[r // mids], g * slots + k) if late else (g, peers[r // mids] * slots + k)
            for d in range(3):
                lev_tab[((late * slots + k) * TOP + s) * 3 + d] = rates[who, d, r % mids * pn.units + unit]

    lax.fori_loop(0, slots, lambda k, c: (look_up(0, k), c)[1], 0)

    cell = lax.broadcasted_iota(jnp.int32, (pn.layers * ny, nz), 0) // ny - halo + p * width
    inside = jnp.logical_and(cell >= 0, cell < pn.total_x)
    coord = (cell.astype(jnp.float32) + 0.5) / pn.total_x
    step_x = 1.0 / pn.total_x
    base, half = TIME_STEP * DIFF / KEEP, 0.5 * TIME_STEP / KEEP
    yi = lax.broadcasted_iota(jnp.int32, (ny, nz), 0)
    zi = lax.broadcasted_iota(jnp.int32, (8, nz), 1)
    y_at = (yi.astype(jnp.float32) + 0.5) / ny
    z_at = (zi.astype(jnp.float32) + 0.5) / nz

    def tables(l, carry):
        lev = levels[l]
        tab_x[l, 0] = jnp.where(inside, base - half * (lev - (coord + step_x)), 0.0)
        tab_x[l, 1] = jnp.where(inside, base + half * (lev - (coord - step_x)), 0.0)
        tab_y[l, 0] = jnp.where(yi < ny - 1, base - half * (lev - (y_at + 1.0 / ny)), 0.0)
        tab_y[l, 1] = jnp.where(yi > 0, base + half * (lev - (y_at - 1.0 / ny)), 0.0)
        tab_z[l, 0] = jnp.where(zi < nz - 1, base - half * (lev - (z_at + 1.0 / nz)), 0.0)
        tab_z[l, 1] = jnp.where(zi > 0, base + half * (lev - (z_at - 1.0 / nz)), 0.0)
        return carry

    lax.fori_loop(0, levels_ref.shape[0], tables, 0)

    def blank(i, carry):
        par, k, s = lax.div(i, slots * TOP), lax.rem(lax.div(i, TOP), slots), lax.rem(i, TOP)
        zero = jnp.zeros((halo * ny, nz), jnp.float32)

        @pl.when(jnp.logical_not(has_left))
        def _():
            near[par, k, s, left_rows] = zero

        @pl.when(jnp.logical_not(has_right))
        def _():
            near[par, k, s, right_rows] = zero

        return carry

    lax.fori_loop(0, 2 * slots * TOP, blank, 0)

    scale = KEEP**SUBSTEPS
    own_cell = lax.broadcasted_iota(jnp.int32, (width, 8, nz), 0) + p * width
    own_x = (own_cell.astype(jnp.float32) + 0.5) / pn.total_x
    hill = 0.1 + own_x * own_x / (0.09 + own_x * own_x)
    for b in range(BLOCKS):
        bit = STATE_BITS - 1 - gene_order[b]
        act = on[bit] * hill
        rate = act + off[bit]
        share = act / rate
        gone = 1.0 - jnp.exp(-rate)
        up = share * gone
        down = (1.0 - share) * gone
        tab_s[b, 0, 0] = (1.0 - up) * scale
        tab_s[b, 0, 1] = down * scale
        tab_s[b, 1, 0] = (1.0 - down) * scale
        tab_s[b, 1, 1] = up * scale

    def spread(src, start, n, c):
        at, size = start * ny, n * ny

        def read(off):
            return src[pl.ds(at + off, size)]

        here = read(0)
        out = here + c[0][pl.ds(at, size)] * read(ny) + c[1][pl.ds(at, size)] * read(-ny)
        by_y, by_z = (n, ny, nz), (size // 8, 8, nz)
        along_y = c[2][None] * read(1).reshape(by_y) + c[3][None] * read(-1).reshape(by_y)
        z_next = pltpu.roll(here, nz - 1, axis=1).reshape(by_z)
        z_last = pltpu.roll(here, 1, axis=1).reshape(by_z)
        along_z = c[4][None] * z_next + c[5][None] * z_last
        return out + along_y.reshape(size, nz) + along_z.reshape(size, nz)

    def diffuse(b, k, batch):
        par, to = lax.rem(b, 2), jnp.minimum(b, 1)
        coef = []
        for m in range(BATCH):
            at = ((to * slots + k) * TOP + batch * BATCH + m) * 3
            lev = [lev_tab[at + d] for d in range(3)]
            coef.append(
                (
                    tab_x.at[lev[0], 0], tab_x.at[lev[0], 1], tab_y[lev[1], 0], tab_y[lev[1], 1],
                    tab_z[lev[2], 0], tab_z[lev[2], 1],
                )
            )
        for i in range(SUBSTEPS):
            extra = SUBSTEPS - 1 - i
            start, stop = halo - extra, halo + width + extra
            for at in range(start, stop, PIECE):
                n = min(PIECE, stop - at)
                for m in range(BATCH):
                    s = batch * BATCH + m
                    src = near.at[par, k, s] if i == 0 else work.at[(i + 1) % 2, m]
                    new = spread(src, at, n, coef[m])
                    if i < SUBSTEPS - 1:
                        work[i % 2, m, rows(at, n)] = new
                    else:
                        post[to, k, s, rows(at - halo, n)] = new

    def move(k, s):
        return pltpu.make_async_remote_copy(
            src_ref=post.at[0, k, s],
            dst_ref=post.at[1, k, s],
            send_sem=move_send,
            recv_sem=move_recv.at[k],
            device_id=(peers[ORDER[s] // mids], p),
            device_id_type=MESH,
        )

    def picked(b):
        order = gene_order[b]
        picks = [order == q for q in range(BLOCKS)]

        def of_mask(values):
            out = values[-1]
            for q in range(BLOCKS - 1):
                out = lax.select(picks[q], values[q], out)
            return out

        return of_mask

    def is_high(of_mask, r):
        values = []
        for mask in MASKS:
            bit = jnp.int32(1 if r & mask else 0)
            if mask >= mids:
                mine = lax.rem(lax.div(g, mask // mids), 2)
                bit = 1 - mine if r & mask else mine
            values.append(bit)
        return of_mask(values)

    def mix(b, k, states, store):
        of_mask = picked(b)
        high = {r: is_high(of_mask, r) for r in states}
        wanted = [r for r in range(TOP) if r in states or any(r ^ mask in states for mask in MASKS)]

        def strip(i, c):
            layer = lax.div(i * 8, ny)
            at = pl.multiple_of(i * 8, 8)
            held = {r: post[1, k, ORDER.index(r), pl.ds(at, 8)] for r in wanted}
            for r in states:
                mate = of_mask([held[r ^ mask] for mask in MASKS])
                store(r, at, tab_s[b, high[r], 0, layer] * held[r] + tab_s[b, high[r], 1, layer] * mate)
            return c

        lax.fori_loop(0, width * ny // 8, strip, 0)

    def place(par, k):
        def store(r, at, value):
            near[par, k, ORDER.index(r), pl.ds(pl.multiple_of(halo * ny + at, 8), 8)] = value

        return store

    def switch(i, carry):
        b, k = lax.div(i, slots), lax.rem(i, slots)
        par = lax.rem(b + 1, 2)

        @pl.when(b == 0)
        def _():
            dst = post.at[1, k, pl.ds(0, away)]
            pltpu.make_async_copy(dst, dst, move_recv.at[k]).wait()

        pl.when(b > 0)(lambda: sent_edges(par, k))
        mix(b, k, list(range(TOP)), place(par, k))
        lax.fori_loop(0, batches, lambda batch, c: (send_edges(par, k, batch), c)[1], 0)
        return carry

    end_par = BLOCKS % 2

    def out_copy(k, r):
        return pltpu.make_async_remote_copy(
            src_ref=near.at[end_par, k, ORDER.index(r), own],
            dst_ref=out_ref.at[r % mids, g * slots + k],
            send_sem=out_send,
            recv_sem=out_recv,
            device_id=(peers[r // mids], p),
            device_id_type=MESH,
        )

    def finish_states(k, states):
        sent = [r for r in states if r >= mids]
        kept = [r for r in states if r < mids]
        if sent:
            mix(BLOCKS - 1, k, sent, place(end_par, k))
            for r in sent:
                out_copy(k, r).start()

        def keep(r, at, value):
            out_ref[r, g * slots + k, pl.ds(at, 8)] = value

        if kept:
            mix(BLOCKS - 1, k, kept, keep)

    finals = final_after()
    opening = min(i for i in range(batches) if finals[i])

    def sub(b, k, batch):
        take_edges(lax.rem(b, 2), k, batch)
        first = b == 0

        @pl.when(first)
        def _():
            dst = near.at[0, k, pl.ds(batch * BATCH, BATCH), own]
            pltpu.make_async_copy(dst, dst, own_sem.at[k, batch]).wait()

        diffuse(b, k, batch)
        for i in range(batches):

            @pl.when(jnp.logical_and(first, batch == i))
            def _(i=i):
                for s in range(i * BATCH, (i + 1) * BATCH):
                    if ORDER[s] >= mids:
                        move(k, s).start()
                    else:
                        post[1, k, s] = post[0, k, s]

            if finals[i]:

                @pl.when(jnp.logical_and(b == BLOCKS - 1, batch == i))
                def _(i=i):
                    if i == opening:
                        sent_edges(end_par, k)
                    finish_states(k, finals[i])

    def step(i, carry):
        b, k = lax.div(i, slots), lax.rem(i, slots)
        lax.fori_loop(0, batches, lambda batch, c: (sub(b, k, batch), c)[1], 0)

        @pl.when(i == slots - 1)
        def _():
            for d in range(1, genes):
                dst = rates.at[peers[d]]
                pltpu.make_async_copy(dst, dst, rate_recv.at[d]).wait()
            lax.fori_loop(0, slots, lambda q, c: (look_up(1, q), c)[1], 0)

        first, last, end = b == 0, k == slots - 1, b == BLOCKS - 1
        start = jnp.where(first, jnp.maximum(k - 1, 0), i)
        stop = jnp.where(first, jnp.where(last, k + 1, k), jnp.where(end, i, i + 1))
        lax.fori_loop(start, stop, switch, 0)
        return carry

    lax.fori_loop(0, BLOCKS * slots, step, 0)

    lax.fori_loop(0, slots, lambda k, c: (sent_edges(1 - end_par, k), c)[1], 0)
    src = post.at[0, :, pl.ds(0, away)]
    pltpu.make_async_copy(src, src, move_send).wait()
    for d in range(1, genes):
        rate_copy(d).wait_send()
    src = near.at[end_par, :, pl.ds(0, away), own]
    pltpu.make_async_copy(src, src, out_send).wait()
    dst = out_ref.at[:, pl.ds(0, (genes - 1) * slots)]
    pltpu.make_async_copy(dst, dst, out_recv).wait()


def local(density, levels, rate_index, on_rate, off_rate, gene_order):
    count, width_x, size_y, size_z = density.shape
    pn = Plan(lax.axis_size("gene"), lax.axis_size("prot"), count, width_x, size_y, size_z)
    shape = (pn.mids, pn.units, width_x * size_y, size_z)
    inputs = (density.reshape(shape), rate_index.T, levels, on_rate, off_rate, gene_order)
    f32, i32 = jnp.float32, jnp.int32
    tall = (pn.layers * size_y, size_z)
    dma = pltpu.SemaphoreType.DMA
    out = pl.pallas_call(
        partial(body, pn),
        out_shape=pltpu.VMEM(shape, f32),
        in_specs=[pl.BlockSpec(memory_space=pltpu.HBM)] * len(inputs),
        out_specs=pl.BlockSpec(memory_space=pltpu.VMEM),
        scratch_shapes=[
            pltpu.VMEM((2, pn.slots, TOP) + tall, f32),
            pltpu.VMEM((2, pn.slots, TOP, width_x * size_y, size_z), f32),
            pltpu.VMEM((2, BATCH) + tall, f32),
            pltpu.VMEM(levels.shape + (2,) + tall, f32),
            pltpu.VMEM(levels.shape + (2, size_y, size_z), f32),
            pltpu.VMEM(levels.shape + (2, 8, size_z), f32),
            pltpu.VMEM((BLOCKS, 2, 2, width_x, 8, size_z), f32),
            pltpu.SMEM((pn.genes, 3, count), i32),
            pltpu.SMEM(levels.shape, f32),
            pltpu.SMEM(on_rate.shape, f32),
            pltpu.SMEM(off_rate.shape, f32),
            pltpu.SMEM(gene_order.shape, i32),
            pltpu.SMEM((2 * pn.slots * TOP * 3,), i32),
            dma((len(inputs) - 1,)),
            dma((pn.slots, TOP // BATCH)),
            dma((2, 2, pn.slots)),
            dma((2, 2, pn.slots, TOP // BATCH)),
            dma(()),
            dma((pn.slots,)),
            dma(()),
            dma(()),
            dma((pn.genes,)),
            dma((pn.genes,)),
        ],
        compiler_params=pltpu.CompilerParams(
            collective_id=0, has_side_effects=True, vmem_limit_bytes=56 * 1024 * 1024
        ),
        name="exchange_evolve",
    )(*[pltpu.with_memory_space_constraint(a, pltpu.HBM) for a in inputs])
    return out.reshape(density.shape)


def solution(mesh):
    in_specs = (P("gene", "prot", None, None), P(), P("gene", None), P(), P(), P())
    out_specs = P("gene", "prot", None, None)
    return jax.shard_map(local, mesh=mesh, in_specs=in_specs, out_specs=out_specs, check_vma=False)
```

time: 158 us -> 150 us (0.949)
  Pallas kernels: 154 us -> 148 us
  local copies, waits for them, and re-layouts: 3.76 us -> 1.67 us
    pallas_call x1, Pallas kernels: 154 us -> 148 us  [local(): pl.pallas_call(partial(body, pn), out_shape=pltpu.VMEM(shape, f32), in_sp...]
    unnamed x1, local copies, waits for them, and re-layouts: 3.76 us -> 1.67 us
where the time goes in v2:
time: 150 us
  Pallas kernels  148 us (99%)
  local copies, waits for them, and re-layouts  1.67 us (1%)
    pallas_call x1, Pallas kernels, local(): pl.pallas_call(partial(body, pn), out_shape=pltpu.VMEM(shape, f32), in_sp...  148 us

profile of v2, /device:TPU:9, one launch (start us, length us, event | category | flops | bytes accessed | tf_op | source)
XLA Modules:
  0.0 149.8 jit_solution(612258005238361358)
XLA Ops:
  0.0 148.1 %exchange_evolve.1 = f32[4,16,96,128]{3,2,1,0:T(8,128)S(1)} custom-call(f32[4,16,96,128]{3,2,1,0:T(8,128)} %bitcast.4, s32[3,64]{1,0:T(4,128)} %bitcast.5, f32[8]{0:T(128)} %levels_ref.1, f32[8]{0:T(128)} %on_ref.1, f32[8]{0:T(128)} %off_ref.1, s32[4]{0:T(128)} %order_ref.1), custom_call_target="tpu_custom_call" | custom-call | tf_op jit(solution)/shard_map/exchange_evolve/pallas_call | solution.py:429
  148.1 1.7 %copy.8 = f32[64,6,16,128]{3,2,1,0:T(8,128)} copy(f32[64,6,16,128]{3,2,1,0:T(8,128)S(1)} %bitcast.3) | data formatting | bytes 6291456

commit v3 on v2

--- a/solution.py
+++ b/solution.py
@@ -15,7 +15,7 @@
 KEEP = 1.0 - 6.0 * TIME_STEP * DIFF
 TOP = 2**BLOCKS
 BATCH = 2
-PIECE = 16
+PIECE = 2
 ORDER = (12, 8, 4, 13, 14, 9, 5, 15, 10, 6, 11, 7, 0, 1, 2, 3)
 MASKS = tuple(TOP >> (q + 1) for q in range(BLOCKS))
 MESH = pl.DeviceIdType.MESH
@@ -44,12 +44,15 @@
 def body(
     pn, x_ref, rate_ref, levels_ref, on_ref, off_ref, order_ref, out_ref,
     near, post, work, tab_x, tab_y, tab_z, tab_s, rates, levels, on, off, gene_order, lev_tab,
-    small_sem, own_sem, halo_send, halo_recv, move_send, move_recv, out_send, out_recv, rate_send, rate_recv,
+    small_sem, own_sem, halo_send, halo_recv, last_recv, move_send, move_recv, out_send, out_recv, rate_send, rate_recv,
 ):
     g, p = lax.axis_index("gene"), lax.axis_index("prot")
     ny, nz = pn.size_y, pn.size_z
     genes, mids, slots, halo, width = pn.genes, pn.mids, pn.slots, pn.halo, pn.width
     has_left, has_right = p > 0, p < pn.prots - 1
+    has_both = jnp.logical_and(has_left, has_right)
+    has_one = jnp.logical_and(jnp.logical_or(has_left, has_right), jnp.logical_not(has_both))
+    near_genes = [1 << i for i in range(genes.bit_length() - 1)]
     batches = TOP // BATCH
     away = (genes - 1) * mids
 
@@ -71,7 +74,7 @@
         pltpu.make_async_copy(src, dst, small_sem.at[i])
         for i, (src, dst) in enumerate(
             [
-                (rate_ref, rates.at[g]), (levels_ref, levels), (on_ref, on), (off_ref, off),
+                (rate_ref, rates.at[0]), (levels_ref, levels), (on_ref, on), (off_ref, off),
                 (order_ref, gene_order),
             ]
         )
@@ -80,7 +83,7 @@
         copy.start()
 
     barrier = pltpu.get_barrier_semaphore()
-    for d in range(1, genes):
+    for d in near_genes:
         pl.semaphore_signal(barrier, inc=1, device_id=(peers[d], p), device_id_type=MESH)
 
     @pl.when(has_left)
@@ -91,41 +94,38 @@
     def _():
         pl.semaphore_signal(barrier, inc=1, device_id=(g, p + 1), device_id_type=MESH)
 
-    pl.semaphore_wait(barrier, genes - 1 + jnp.where(has_left, 1, 0) + jnp.where(has_right, 1, 0))
-
-    def edge(src, par, way, k, batch, where):
+    pl.semaphore_wait(barrier, len(near_genes) + jnp.where(has_left, 1, 0) + jnp.where(has_right, 1, 0))
+
+    def edge(src, par, way, k, where, recv_sem):
         return pltpu.make_async_remote_copy(
             src_ref=src,
             dst_ref=near.at[par, k, where, right_rows if way else left_rows],
-            send_sem=halo_send.at[par, way, k],
-            recv_sem=halo_recv.at[par, way, k, batch],
+            send_sem=halo_send.at[par],
+            recv_sem=recv_sem,
             device_id=(g, p - 1 if way else p + 1),
             device_id_type=MESH,
         )
 
     first_layer = (width - halo, 0)
-    can_send, can_take = (has_right, has_left), (has_left, has_right)
-
-    def send_edges(par, k, batch):
-        where = pl.ds(batch * BATCH, BATCH)
+    can_send = (has_right, has_left)
+
+    def send_edges(par, k, where, recv_sem):
         for way in range(2):
             src = near.at[par, k, where, rows(halo + first_layer[way], halo)]
-            pl.when(can_send[way])(edge(src, par, way, k, batch, where).start)
-
-    def sent_edges(par, k):
-        for way in range(2):
-            src = near.at[par, k, :, left_rows]
-            pl.when(can_send[way])(pltpu.make_async_copy(src, src, halo_send.at[par, way, k]).wait)
-
-    def take_edges(par, k, batch):
-        for way in range(2):
-            dst = near.at[par, k, pl.ds(batch * BATCH, BATCH), right_rows if way else left_rows]
-            pl.when(can_take[way])(pltpu.make_async_copy(dst, dst, halo_recv.at[par, way, k, batch]).wait)
+            pl.when(can_send[way])(edge(src, par, way, k, where, recv_sem).start)
+
+    def both_ways(ref_of, sem):
+        one, two = ref_of(rows(0, halo)), ref_of(rows(0, 2 * halo))
+        pl.when(has_one)(pltpu.make_async_copy(one, one, sem).wait)
+        pl.when(has_both)(pltpu.make_async_copy(two, two, sem).wait)
+
+    def sent_edges(par):
+        both_ways(lambda at: near.at[par, :, :, at], halo_send.at[par])
 
     def own_copy(k, s):
         unit = peers[ORDER[s] // mids] * slots + k
         return pltpu.make_async_copy(
-            x_ref.at[ORDER[s] % mids, unit], near.at[0, k, s, own], own_sem.at[k, s // BATCH]
+            x_ref.at[ORDER[s] % mids, unit], near.at[0, k, s, own], own_sem
         )
 
     def open_slot(k, carry):
@@ -136,7 +136,7 @@
                 for s, r in enumerate(ORDER):
                     unit = peers[r // mids] * slots + k
                     src = x_ref.at[r % mids, unit, rows(first_layer[way], halo)]
-                    edge(src, 0, way, k, s // BATCH, s).start()
+                    edge(src, 0, way, k, s, halo_recv.at[0, k]).start()
 
         for s in range(TOP):
             own_copy(k, s).start()
@@ -146,25 +146,24 @@
     for copy in small:
         copy.wait()
 
-    def rate_copy(d):
+    def rate_copy(i):
         return pltpu.make_async_remote_copy(
-            src_ref=rates.at[g],
-            dst_ref=rates.at[g],
-            send_sem=rate_send.at[d],
-            recv_sem=rate_recv.at[d],
-            device_id=(peers[d], p),
+            src_ref=rates.at[pl.ds(0, near_genes[i])],
+            dst_ref=rates.at[pl.ds(near_genes[i], near_genes[i])],
+            send_sem=rate_send,
+            recv_sem=rate_recv.at[i],
+            device_id=(peers[near_genes[i]], p),
             device_id_type=MESH,
         )
-
-    for d in range(1, genes):
-        rate_copy(d).start()
 
     def look_up(late, k):
         for s, r in enumerate(ORDER):
-            who, unit = (peers[r // mids], g * slots + k) if late else (g, peers[r // mids] * slots + k)
+            row = r // mids if late else 0
+            unit = (g if late else peers[r // mids]) * slots + k
             for d in range(3):
-                lev_tab[((late * slots + k) * TOP + s) * 3 + d] = rates[who, d, r % mids * pn.units + unit]
-
+                lev_tab[((late * slots + k) * TOP + s) * 3 + d] = rates[row, d, r % mids * pn.units + unit]
+
+    rate_copy(0).start()
     lax.fori_loop(0, slots, lambda k, c: (look_up(0, k), c)[1], 0)
 
     cell = lax.broadcasted_iota(jnp.int32, (pn.layers * ny, nz), 0) // ny - halo + p * width
@@ -189,6 +188,10 @@
 
     lax.fori_loop(0, levels_ref.shape[0], tables, 0)
 
+    for i in range(1, len(near_genes)):
+        rate_copy(i - 1).wait_recv()
+        rate_copy(i).start()
+
     def blank(i, carry):
         par, k, s = lax.div(i, slots * TOP), lax.rem(lax.div(i, TOP), slots), lax.rem(i, TOP)
         zero = jnp.zeros((halo * ny, nz), jnp.float32)
@@ -206,7 +209,7 @@
     lax.fori_loop(0, 2 * slots * TOP, blank, 0)
 
     scale = KEEP**SUBSTEPS
-    own_cell = lax.broadcasted_iota(jnp.int32, (width, 8, nz), 0) + p * width
+    own_cell = lax.broadcasted_iota(jnp.int32, (width * ny, nz), 0) // ny + p * width
     own_x = (own_cell.astype(jnp.float32) + 0.5) / pn.total_x
     hill = 0.1 + own_x * own_x / (0.09 + own_x * own_x)
     for b in range(BLOCKS):
@@ -221,6 +224,11 @@
         tab_s[b, 0, 1] = down * scale
         tab_s[b, 1, 0] = (1.0 - down) * scale
         tab_s[b, 1, 1] = up * scale
+
+    rate_copy(len(near_genes) - 1).wait_recv()
+    lax.fori_loop(0, slots, lambda k, c: (look_up(1, k), c)[1], 0)
+    mine = near.at[0, :, :, own]
+    pltpu.make_async_copy(mine, mine, own_sem).wait()
 
     def spread(src, start, n, c):
         at, size = start * ny, n * ny
@@ -300,20 +308,22 @@
         high = {r: is_high(of_mask, r) for r in states}
         wanted = [r for r in range(TOP) if r in states or any(r ^ mask in states for mask in MASKS)]
 
+        span = ny * (2 if width % 2 == 0 and len(states) <= 4 else 1)
+
         def strip(i, c):
-            layer = lax.div(i * 8, ny)
-            at = pl.multiple_of(i * 8, 8)
-            held = {r: post[1, k, ORDER.index(r), pl.ds(at, 8)] for r in wanted}
+            at = pl.multiple_of(i * span, span)
+            cut = pl.ds(at, span)
+            held = {r: post[1, k, ORDER.index(r), cut] for r in wanted}
             for r in states:
                 mate = of_mask([held[r ^ mask] for mask in MASKS])
-                store(r, at, tab_s[b, high[r], 0, layer] * held[r] + tab_s[b, high[r], 1, layer] * mate)
+                store(r, at, span, tab_s[b, high[r], 0, cut] * held[r] + tab_s[b, high[r], 1, cut] * mate)
             return c
 
-        lax.fori_loop(0, width * ny // 8, strip, 0)
+        lax.fori_loop(0, width * ny // span, strip, 0)
 
     def place(par, k):
-        def store(r, at, value):
-            near[par, k, ORDER.index(r), pl.ds(pl.multiple_of(halo * ny + at, 8), 8)] = value
+        def store(r, at, span, value):
+            near[par, k, ORDER.index(r), pl.ds(pl.multiple_of(halo * ny + at, ny), span)] = value
 
         return store
 
@@ -326,9 +336,21 @@
             dst = post.at[1, k, pl.ds(0, away)]
             pltpu.make_async_copy(dst, dst, move_recv.at[k]).wait()
 
-        pl.when(b > 0)(lambda: sent_edges(par, k))
+        pl.when(jnp.logical_and(b > 0, k == 0))(lambda: sent_edges(par))
         mix(b, k, list(range(TOP)), place(par, k))
-        lax.fori_loop(0, batches, lambda batch, c: (send_edges(par, k, batch), c)[1], 0)
+
+        @pl.when(b < BLOCKS - 2)
+        def _():
+            send_edges(par, k, pl.ds(0, TOP), halo_recv.at[par, k])
+
+        @pl.when(b == BLOCKS - 2)
+        def _():
+            def each(batch, c):
+                send_edges(par, k, pl.ds(batch * BATCH, BATCH), last_recv.at[k, batch])
+                return c
+
+            lax.fori_loop(0, batches, each, 0)
+
         return carry
 
     end_par = BLOCKS % 2
@@ -351,8 +373,8 @@
             for r in sent:
                 out_copy(k, r).start()
 
-        def keep(r, at, value):
-            out_ref[r, g * slots + k, pl.ds(at, 8)] = value
+        def keep(r, at, span, value):
+            out_ref[r, g * slots + k, pl.ds(at, span)] = value
 
         if kept:
             mix(BLOCKS - 1, k, kept, keep)
@@ -361,13 +383,15 @@
     opening = min(i for i in range(batches) if finals[i])
 
     def sub(b, k, batch):
-        take_edges(lax.rem(b, 2), k, batch)
-        first = b == 0
-
-        @pl.when(first)
-        def _():
-            dst = near.at[0, k, pl.ds(batch * BATCH, BATCH), own]
-            pltpu.make_async_copy(dst, dst, own_sem.at[k, batch]).wait()
+        first, end, par = b == 0, b == BLOCKS - 1, lax.rem(b, 2)
+
+        @pl.when(jnp.logical_and(jnp.logical_not(end), batch == 0))
+        def _():
+            both_ways(lambda at: near.at[par, k, :, at], halo_recv.at[par, k])
+
+        @pl.when(end)
+        def _():
+            both_ways(lambda at: near.at[par, k, pl.ds(batch * BATCH, BATCH), at], last_recv.at[k, batch])
 
         diffuse(b, k, batch)
         for i in range(batches):
@@ -382,22 +406,15 @@
 
             if finals[i]:
 
-                @pl.when(jnp.logical_and(b == BLOCKS - 1, batch == i))
+                @pl.when(jnp.logical_and(end, batch == i))
                 def _(i=i):
                     if i == opening:
-                        sent_edges(end_par, k)
+                        pl.when(k == 0)(lambda: sent_edges(end_par))
                     finish_states(k, finals[i])
 
     def step(i, carry):
         b, k = lax.div(i, slots), lax.rem(i, slots)
         lax.fori_loop(0, batches, lambda batch, c: (sub(b, k, batch), c)[1], 0)
-
-        @pl.when(i == slots - 1)
-        def _():
-            for d in range(1, genes):
-                dst = rates.at[peers[d]]
-                pltpu.make_async_copy(dst, dst, rate_recv.at[d]).wait()
-            lax.fori_loop(0, slots, lambda q, c: (look_up(1, q), c)[1], 0)
 
         first, last, end = b == 0, k == slots - 1, b == BLOCKS - 1
         start = jnp.where(first, jnp.maximum(k - 1, 0), i)
@@ -407,11 +424,11 @@
 
     lax.fori_loop(0, BLOCKS * slots, step, 0)
 
-    lax.fori_loop(0, slots, lambda k, c: (sent_edges(1 - end_par, k), c)[1], 0)
+    sent_edges(1 - end_par)
     src = post.at[0, :, pl.ds(0, away)]
     pltpu.make_async_copy(src, src, move_send).wait()
-    for d in range(1, genes):
-        rate_copy(d).wait_send()
+    src = rates.at[pl.ds(0, genes - 1)]
+    pltpu.make_async_copy(src, src, rate_send).wait()
     src = near.at[end_par, :, pl.ds(0, away), own]
     pltpu.make_async_copy(src, src, out_send).wait()
     dst = out_ref.at[:, pl.ds(0, (genes - 1) * slots)]
@@ -438,7 +455,7 @@
             pltpu.VMEM(levels.shape + (2,) + tall, f32),
             pltpu.VMEM(levels.shape + (2, size_y, size_z), f32),
             pltpu.VMEM(levels.shape + (2, 8, size_z), f32),
-            pltpu.VMEM((BLOCKS, 2, 2, width_x, 8, size_z), f32),
+            pltpu.VMEM((BLOCKS, 2, 2, width_x * size_y, size_z), f32),
             pltpu.SMEM((pn.genes, 3, count), i32),
             pltpu.SMEM(levels.shape, f32),
             pltpu.SMEM(on_rate.shape, f32),
@@ -446,15 +463,16 @@
             pltpu.SMEM(gene_order.shape, i32),
             pltpu.SMEM((2 * pn.slots * TOP * 3,), i32),
             dma((len(inputs) - 1,)),
+            dma(()),
+            dma((2,)),
+            dma((2, pn.slots)),
             dma((pn.slots, TOP // BATCH)),
-            dma((2, 2, pn.slots)),
-            dma((2, 2, pn.slots, TOP // BATCH)),
             dma(()),
             dma((pn.slots,)),
             dma(()),
             dma(()),
-            dma((pn.genes,)),
-            dma((pn.genes,)),
+            dma(()),
+            dma((pn.genes.bit_length() - 1,)),
         ],
         compiler_params=pltpu.CompilerParams(
             collective_id=0, has_side_effects=True, vmem_limit_bytes=56 * 1024 * 1024

time: 150 us -> 154 us (1.027)
  Pallas kernels: 148 us -> 152 us
    pallas_call x1, Pallas kernels: 148 us -> 152 us  [local(): pl.pallas_call(partial(body, pn), out_shape=pltpu.VMEM(shape, f32), in_sp...]
where the time goes in v3:
time: 154 us
  Pallas kernels  152 us (99%)
  local copies, waits for them, and re-layouts  1.67 us (1%)
    pallas_call x1, Pallas kernels, local(): pl.pallas_call(partial(body, pn), out_shape=pltpu.VMEM(shape, f32), in_sp...  152 us

profile of v3, /device:TPU:9, one launch (start us, length us, event | category | flops | bytes accessed | tf_op | source)
XLA Modules:
  0.0 153.8 jit_solution(10446722378095718329)
XLA Ops:
  0.0 152.1 %exchange_evolve.1 = f32[4,16,96,128]{3,2,1,0:T(8,128)S(1)} custom-call(f32[4,16,96,128]{3,2,1,0:T(8,128)} %bitcast.4, s32[3,64]{1,0:T(4,128)} %bitcast.5, f32[8]{0:T(128)} %levels_ref.1, f32[8]{0:T(128)} %on_ref.1, f32[8]{0:T(128)} %off_ref.1, s32[4]{0:T(128)} %order_ref.1), custom_call_target="tpu_custom_call" | custom-call | tf_op jit(solution)/shard_map/exchange_evolve/pallas_call | solution.py:446
  152.1 1.7 %copy.8 = f32[64,6,16,128]{3,2,1,0:T(8,128)} copy(f32[64,6,16,128]{3,2,1,0:T(8,128)S(1)} %bitcast.3) | data formatting | bytes 6291456

commit v4 on v3

--- a/solution.py
+++ b/solution.py
@@ -15,7 +15,7 @@
 KEEP = 1.0 - 6.0 * TIME_STEP * DIFF
 TOP = 2**BLOCKS
 BATCH = 2
-PIECE = 2
+PIECE = 1
 ORDER = (12, 8, 4, 13, 14, 9, 5, 15, 10, 6, 11, 7, 0, 1, 2, 3)
 MASKS = tuple(TOP >> (q + 1) for q in range(BLOCKS))
 MESH = pl.DeviceIdType.MESH
@@ -53,7 +53,8 @@
     has_both = jnp.logical_and(has_left, has_right)
     has_one = jnp.logical_and(jnp.logical_or(has_left, has_right), jnp.logical_not(has_both))
     near_genes = [1 << i for i in range(genes.bit_length() - 1)]
-    batches = TOP // BATCH
+    batches, part = TOP // BATCH, TOP // 2
+    fine = max((BLOCKS - 1) * slots - 2, slots)
     away = (genes - 1) * mids
 
     def rows(layer, n):
@@ -136,7 +137,7 @@
                 for s, r in enumerate(ORDER):
                     unit = peers[r // mids] * slots + k
                     src = x_ref.at[r % mids, unit, rows(first_layer[way], halo)]
-                    edge(src, 0, way, k, s, halo_recv.at[0, k]).start()
+                    edge(src, 0, way, k, s, halo_recv.at[0, k, s // part]).start()
 
         for s in range(TOP):
             own_copy(k, s).start()
@@ -339,14 +340,15 @@
         pl.when(jnp.logical_and(b > 0, k == 0))(lambda: sent_edges(par))
         mix(b, k, list(range(TOP)), place(par, k))
 
-        @pl.when(b < BLOCKS - 2)
-        def _():
-            send_edges(par, k, pl.ds(0, TOP), halo_recv.at[par, k])
-
-        @pl.when(b == BLOCKS - 2)
+        @pl.when(i + slots < fine)
+        def _():
+            for h in range(2):
+                send_edges(par, k, pl.ds(h * part, part), halo_recv.at[par, k, h])
+
+        @pl.when(jnp.logical_and(i + slots >= fine, b < BLOCKS - 1))
         def _():
             def each(batch, c):
-                send_edges(par, k, pl.ds(batch * BATCH, BATCH), last_recv.at[k, batch])
+                send_edges(par, k, pl.ds(batch * BATCH, BATCH), last_recv.at[i + slots - fine, batch])
                 return c
 
             lax.fori_loop(0, batches, each, 0)
@@ -385,13 +387,16 @@
     def sub(b, k, batch):
         first, end, par = b == 0, b == BLOCKS - 1, lax.rem(b, 2)
 
-        @pl.when(jnp.logical_and(jnp.logical_not(end), batch == 0))
-        def _():
-            both_ways(lambda at: near.at[par, k, :, at], halo_recv.at[par, k])
-
-        @pl.when(end)
-        def _():
-            both_ways(lambda at: near.at[par, k, pl.ds(batch * BATCH, BATCH), at], last_recv.at[k, batch])
+        item = b * slots + k
+        h = lax.div(batch * BATCH, part)
+
+        @pl.when(jnp.logical_and(item < fine, lax.rem(batch * BATCH, part) == 0))
+        def _():
+            both_ways(lambda at: near.at[par, k, pl.ds(h * part, part), at], halo_recv.at[par, k, h])
+
+        @pl.when(item >= fine)
+        def _():
+            both_ways(lambda at: near.at[par, k, pl.ds(batch * BATCH, BATCH), at], last_recv.at[item - fine, batch])
 
         diffuse(b, k, batch)
         for i in range(batches):
@@ -465,8 +470,8 @@
             dma((len(inputs) - 1,)),
             dma(()),
             dma((2,)),
-            dma((2, pn.slots)),
-            dma((pn.slots, TOP // BATCH)),
+            dma((2, pn.slots, 2)),
+            dma((pn.slots + 2, TOP // BATCH)),
             dma(()),
             dma((pn.slots,)),
             dma(()),

time: 154 us -> 149 us (0.968)
  Pallas kernels: 152 us -> 147 us
    pallas_call x1, Pallas kernels: 152 us -> 147 us  [local(): pl.pallas_call(partial(body, pn), out_shape=pltpu.VMEM(shape, f32), in_sp...]
where the time goes in v4:
time: 149 us
  Pallas kernels  147 us (99%)
  local copies, waits for them, and re-layouts  1.67 us (1%)
    pallas_call x1, Pallas kernels, local(): pl.pallas_call(partial(body, pn), out_shape=pltpu.VMEM(shape, f32), in_sp...  147 us

profile of v4, /device:TPU:9, one launch (start us, length us, event | category | flops | bytes accessed | tf_op | source)
XLA Modules:
  0.0 148.6 jit_solution(13902005025477890176)
XLA Ops:
  0.0 146.9 %exchange_evolve.1 = f32[4,16,96,128]{3,2,1,0:T(8,128)S(1)} custom-call(f32[4,16,96,128]{3,2,1,0:T(8,128)} %bitcast.4, s32[3,64]{1,0:T(4,128)} %bitcast.5, f32[8]{0:T(128)} %levels_ref.1, f32[8]{0:T(128)} %on_ref.1, f32[8]{0:T(128)} %off_ref.1, s32[4]{0:T(128)} %order_ref.1), custom_call_target="tpu_custom_call" | custom-call | tf_op jit(solution)/shard_map/exchange_evolve/pallas_call | solution.py:451
  146.9 1.7 %copy.8 = f32[64,6,16,128]{3,2,1,0:T(8,128)} copy(f32[64,6,16,128]{3,2,1,0:T(8,128)S(1)} %bitcast.3) | data formatting | bytes 6291456

commit v5 on v4

--- a/solution.py
+++ b/solution.py
@@ -16,15 +16,16 @@
 TOP = 2**BLOCKS
 BATCH = 2
 PIECE = 1
+QUAD = 4
 ORDER = (12, 8, 4, 13, 14, 9, 5, 15, 10, 6, 11, 7, 0, 1, 2, 3)
 MASKS = tuple(TOP >> (q + 1) for q in range(BLOCKS))
 MESH = pl.DeviceIdType.MESH
 
 
 def final_after():
-    batch_of = {r: s // BATCH for s, r in enumerate(ORDER)}
+    batch_of = {r: s // QUAD for s, r in enumerate(ORDER)}
     last = {r: max(batch_of[a] for a in [r] + [r ^ mask for mask in MASKS]) for r in range(TOP)}
-    return [[r for r in ORDER if last[r] == i] for i in range(TOP // BATCH)]
+    return [[r for r in ORDER if last[r] == i] for i in range(TOP // QUAD)]
 
 
 class Plan:
@@ -38,7 +39,7 @@
         self.halo = SUBSTEPS
         self.layers = width + 2 * self.halo
         assert self.slots * genes == self.units and self.mids * genes == TOP
-        assert width >= self.halo
+        assert width == self.halo and self.halo % 2 == 0
 
 
 def body(
@@ -53,7 +54,9 @@
     has_both = jnp.logical_and(has_left, has_right)
     has_one = jnp.logical_and(jnp.logical_or(has_left, has_right), jnp.logical_not(has_both))
     near_genes = [1 << i for i in range(genes.bit_length() - 1)]
-    batches, part = TOP // BATCH, TOP // 2
+    batches, quads, part = TOP // BATCH, TOP // QUAD, TOP // 2
+    near_half = halo // 2
+    even = lax.rem(p, 2) == 0
     fine = max((BLOCKS - 1) * slots - 2, slots)
     away = (genes - 1) * mids
 
@@ -114,6 +117,43 @@
         for way in range(2):
             src = near.at[par, k, where, rows(halo + first_layer[way], halo)]
             pl.when(can_send[way])(edge(src, par, way, k, where, recv_sem).start)
+
+    def slow(way):
+        return even if way else jnp.logical_not(even)
+
+    def send_turn(par, k, turn, quad, recv_sem):
+        where = pl.ds(quad * QUAD, QUAD)
+        for way in range(2):
+            skip = near_half * (turn if way else 1 - turn)
+            to = halo + width if way else 0
+            half_copy = pltpu.make_async_remote_copy(
+                src_ref=near.at[par, k, where, rows(halo + skip, near_half)],
+                dst_ref=near.at[par, k, where, rows(to + skip, near_half)],
+                send_sem=halo_send.at[par],
+                recv_sem=recv_sem,
+                device_id=(g, p - 1 if way else p + 1),
+                device_id_type=MESH,
+            )
+            src = near.at[par, k, where, own]
+            whole = edge(src, par, way, k, where, recv_sem)
+            there = jnp.logical_and(can_send[way], slow(way))
+            pl.when(there)(half_copy.start)
+            there = jnp.logical_and(can_send[way], jnp.logical_not(slow(way)))
+            pl.when(jnp.logical_and(there, turn == 0))(whole.start)
+
+    has_slow = jnp.logical_or(jnp.logical_and(even, has_left), jnp.logical_and(jnp.logical_not(even), has_right))
+    has_fast = jnp.logical_or(jnp.logical_and(even, has_right), jnp.logical_and(jnp.logical_not(even), has_left))
+
+    def take_turn(par, k, turn, quad, sem):
+        def await_layers(n):
+            ref = near.at[par, k, pl.ds(quad * QUAD, QUAD), rows(0, n)]
+            return pltpu.make_async_copy(ref, ref, sem).wait
+
+        opening_turn = turn == 0
+        pl.when(jnp.logical_and(opening_turn, jnp.logical_and(has_slow, has_fast)))(await_layers(halo + near_half))
+        pl.when(jnp.logical_and(opening_turn, jnp.logical_and(jnp.logical_not(has_slow), has_fast)))(await_layers(halo))
+        pl.when(jnp.logical_and(opening_turn, jnp.logical_and(has_slow, jnp.logical_not(has_fast))))(await_layers(near_half))
+        pl.when(jnp.logical_and(turn == 1, has_slow))(await_layers(near_half))
 
     def both_ways(ref_of, sem):
         one, two = ref_of(rows(0, halo)), ref_of(rows(0, 2 * halo))
@@ -233,12 +273,17 @@
 
     def spread(src, start, n, c):
         at, size = start * ny, n * ny
+        fixed = isinstance(start, int)
+
+        def cut(off):
+            to = at + off
+            return pl.ds(to if fixed or off % ny else pl.multiple_of(to, ny), size)
 
         def read(off):
-            return src[pl.ds(at + off, size)]
+            return src[cut(off)]
 
         here = read(0)
-        out = here + c[0][pl.ds(at, size)] * read(ny) + c[1][pl.ds(at, size)] * read(-ny)
+        out = here + c[0][cut(0)] * read(ny) + c[1][cut(0)] * read(-ny)
         by_y, by_z = (n, ny, nz), (size // 8, 8, nz)
         along_y = c[2][None] * read(1).reshape(by_y) + c[3][None] * read(-1).reshape(by_y)
         z_next = pltpu.roll(here, nz - 1, axis=1).reshape(by_z)
@@ -246,11 +291,10 @@
         along_z = c[4][None] * z_next + c[5][None] * z_last
         return out + along_y.reshape(size, nz) + along_z.reshape(size, nz)
 
-    def diffuse(b, k, batch):
-        par, to = lax.rem(b, 2), jnp.minimum(b, 1)
+    def diffuse(par, to, k, first, count, skip, cells):
         coef = []
-        for m in range(BATCH):
-            at = ((to * slots + k) * TOP + batch * BATCH + m) * 3
+        for m in range(count):
+            at = ((to * slots + k) * TOP + first + m) * 3
             lev = [lev_tab[at + d] for d in range(3)]
             coef.append(
                 (
@@ -258,19 +302,21 @@
                     tab_z[lev[2], 0], tab_z[lev[2], 1],
                 )
             )
+
+        def lay(layer, n):
+            return rows(layer, n) if isinstance(layer, int) else pl.ds(pl.multiple_of(layer * ny, ny), n * ny)
+
         for i in range(SUBSTEPS):
             extra = SUBSTEPS - 1 - i
-            start, stop = halo - extra, halo + width + extra
-            for at in range(start, stop, PIECE):
-                n = min(PIECE, stop - at)
-                for m in range(BATCH):
-                    s = batch * BATCH + m
-                    src = near.at[par, k, s] if i == 0 else work.at[(i + 1) % 2, m]
-                    new = spread(src, at, n, coef[m])
+            for at in range(-extra, cells + extra, PIECE):
+                n = min(PIECE, cells + extra - at)
+                for m in range(count):
+                    src = near.at[par, k, first + m] if i == 0 else work.at[(i + 1) % 2, m]
+                    new = spread(src, halo + skip + at, n, coef[m])
                     if i < SUBSTEPS - 1:
-                        work[i % 2, m, rows(at, n)] = new
+                        work[i % 2, m, lay(halo + skip + at, n)] = new
                     else:
-                        post[to, k, s, rows(at - halo, n)] = new
+                        post[to, k, first + m, lay(skip + at, n)] = new
 
     def move(k, s):
         return pltpu.make_async_remote_copy(
@@ -304,15 +350,15 @@
             values.append(bit)
         return of_mask(values)
 
-    def mix(b, k, states, store):
+    def mix(b, k, states, store, skip=0, cells=width):
         of_mask = picked(b)
         high = {r: is_high(of_mask, r) for r in states}
         wanted = [r for r in range(TOP) if r in states or any(r ^ mask in states for mask in MASKS)]
 
-        span = ny * (2 if width % 2 == 0 and len(states) <= 4 else 1)
+        span = ny
 
         def strip(i, c):
-            at = pl.multiple_of(i * span, span)
+            at = pl.multiple_of((skip + i) * span, span)
             cut = pl.ds(at, span)
             held = {r: post[1, k, ORDER.index(r), cut] for r in wanted}
             for r in states:
@@ -320,7 +366,7 @@
                 store(r, at, span, tab_s[b, high[r], 0, cut] * held[r] + tab_s[b, high[r], 1, cut] * mate)
             return c
 
-        lax.fori_loop(0, width * ny // span, strip, 0)
+        lax.fori_loop(0, cells, strip, 0)
 
     def place(par, k):
         def store(r, at, span, value):
@@ -345,7 +391,7 @@
             for h in range(2):
                 send_edges(par, k, pl.ds(h * part, part), halo_recv.at[par, k, h])
 
-        @pl.when(jnp.logical_and(i + slots >= fine, b < BLOCKS - 1))
+        @pl.when(jnp.logical_and(i + slots >= fine, b < BLOCKS - 2))
         def _():
             def each(batch, c):
                 send_edges(par, k, pl.ds(batch * BATCH, BATCH), last_recv.at[i + slots - fine, batch])
@@ -353,40 +399,48 @@
 
             lax.fori_loop(0, batches, each, 0)
 
+        @pl.when(b == BLOCKS - 2)
+        def _():
+            def turn(t, c):
+                send_turn(par, k, lax.div(t, quads), lax.rem(t, quads), last_recv.at[i + slots - fine, t])
+                return c
+
+            lax.fori_loop(0, 2 * quads, turn, 0)
+
         return carry
 
     end_par = BLOCKS % 2
 
-    def out_copy(k, r):
+    def out_copy(k, r, skip):
+        at = pl.multiple_of(skip * ny, ny)
         return pltpu.make_async_remote_copy(
-            src_ref=near.at[end_par, k, ORDER.index(r), own],
-            dst_ref=out_ref.at[r % mids, g * slots + k],
+            src_ref=near.at[end_par, k, ORDER.index(r), pl.ds(halo * ny + at, near_half * ny)],
+            dst_ref=out_ref.at[r % mids, g * slots + k, pl.ds(at, near_half * ny)],
             send_sem=out_send,
             recv_sem=out_recv,
             device_id=(peers[r // mids], p),
             device_id_type=MESH,
         )
 
-    def finish_states(k, states):
+    def finish_states(k, states, skip):
         sent = [r for r in states if r >= mids]
         kept = [r for r in states if r < mids]
         if sent:
-            mix(BLOCKS - 1, k, sent, place(end_par, k))
+            mix(BLOCKS - 1, k, sent, place(end_par, k), skip, near_half)
             for r in sent:
-                out_copy(k, r).start()
+                out_copy(k, r, skip).start()
 
         def keep(r, at, span, value):
             out_ref[r, g * slots + k, pl.ds(at, span)] = value
 
         if kept:
-            mix(BLOCKS - 1, k, kept, keep)
+            mix(BLOCKS - 1, k, kept, keep, skip, near_half)
 
     finals = final_after()
-    opening = min(i for i in range(batches) if finals[i])
+    opening = min(i for i in range(quads) if finals[i])
 
     def sub(b, k, batch):
-        first, end, par = b == 0, b == BLOCKS - 1, lax.rem(b, 2)
-
+        first, par = b == 0, lax.rem(b, 2)
         item = b * slots + k
         h = lax.div(batch * BATCH, part)
 
@@ -398,7 +452,7 @@
         def _():
             both_ways(lambda at: near.at[par, k, pl.ds(batch * BATCH, BATCH), at], last_recv.at[item - fine, batch])
 
-        diffuse(b, k, batch)
+        diffuse(par, jnp.minimum(b, 1), k, batch * BATCH, BATCH, 0, width)
         for i in range(batches):
 
             @pl.when(jnp.logical_and(first, batch == i))
@@ -409,25 +463,37 @@
                     else:
                         post[1, k, s] = post[0, k, s]
 
+    def last_sub(k, t):
+        turn, quad, par = lax.div(t, quads), lax.rem(t, quads), 1 - end_par
+        skip = near_half * jnp.where(even, 1 - turn, turn)
+        take_turn(par, k, turn, quad, last_recv.at[(BLOCKS - 1) * slots - fine + k, t])
+        diffuse(par, 1, k, quad * QUAD, QUAD, skip, near_half)
+        for i in range(quads):
             if finals[i]:
 
-                @pl.when(jnp.logical_and(end, batch == i))
+                @pl.when(quad == i)
                 def _(i=i):
                     if i == opening:
-                        pl.when(k == 0)(lambda: sent_edges(end_par))
-                    finish_states(k, finals[i])
+                        pl.when(jnp.logical_and(k == 0, turn == 0))(lambda: sent_edges(end_par))
+                    finish_states(k, finals[i], skip)
 
     def step(i, carry):
         b, k = lax.div(i, slots), lax.rem(i, slots)
         lax.fori_loop(0, batches, lambda batch, c: (sub(b, k, batch), c)[1], 0)
 
-        first, last, end = b == 0, k == slots - 1, b == BLOCKS - 1
+        first, last = b == 0, k == slots - 1
         start = jnp.where(first, jnp.maximum(k - 1, 0), i)
-        stop = jnp.where(first, jnp.where(last, k + 1, k), jnp.where(end, i, i + 1))
+        stop = jnp.where(first, jnp.where(last, k + 1, k), i + 1)
         lax.fori_loop(start, stop, switch, 0)
         return carry
 
-    lax.fori_loop(0, BLOCKS * slots, step, 0)
+    lax.fori_loop(0, (BLOCKS - 1) * slots, step, 0)
+
+    def last_step(i, carry):
+        last_sub(lax.div(i, 2 * quads), lax.rem(i, 2 * quads))
+        return carry
+
+    lax.fori_loop(0, slots * 2 * quads, last_step, 0)
 
     sent_edges(1 - end_par)
     src = post.at[0, :, pl.ds(0, away)]
@@ -456,7 +522,7 @@
         scratch_shapes=[
             pltpu.VMEM((2, pn.slots, TOP) + tall, f32),
             pltpu.VMEM((2, pn.slots, TOP, width_x * size_y, size_z), f32),
-            pltpu.VMEM((2, BATCH) + tall, f32),
+            pltpu.VMEM((2, QUAD) + tall, f32),
             pltpu.VMEM(levels.shape + (2,) + tall, f32),
             pltpu.VMEM(levels.shape + (2, size_y, size_z), f32),
             pltpu.VMEM(levels.shape + (2, 8, size_z), f32),

time: 149 us -> 148 us (level)
  no operation moved by 1% of the time
where the time goes in v5:
time: 148 us
  Pallas kernels  146 us (99%)
  local copies, waits for them, and re-layouts  1.67 us (1%)
    pallas_call x1, Pallas kernels, local(): pl.pallas_call(partial(body, pn), out_shape=pltpu.VMEM(shape, f32), in_sp...  146 us

profile of v5, /device:TPU:9, one launch (start us, length us, event | category | flops | bytes accessed | tf_op | source)
XLA Modules:
  0.0 148.0 jit_solution(10146071741576835140)
XLA Ops:
  0.0 146.4 %exchange_evolve.1 = f32[4,16,96,128]{3,2,1,0:T(8,128)S(1)} custom-call(f32[4,16,96,128]{3,2,1,0:T(8,128)} %bitcast.4, s32[3,64]{1,0:T(4,128)} %bitcast.5, f32[8]{0:T(128)} %levels_ref.1, f32[8]{0:T(128)} %on_ref.1, f32[8]{0:T(128)} %off_ref.1, s32[4]{0:T(128)} %order_ref.1), custom_call_target="tpu_custom_call" | custom-call | tf_op jit(solution)/shard_map/exchange_evolve/pallas_call | solution.py:517
  146.4 1.7 %copy.8 = f32[64,6,16,128]{3,2,1,0:T(8,128)} copy(f32[64,6,16,128]{3,2,1,0:T(8,128)S(1)} %bitcast.3) | data formatting | bytes 6291456

commit v6 on v5

--- a/solution.py
+++ b/solution.py
@@ -14,7 +14,7 @@
 TIME_STEP = 0.15
 KEEP = 1.0 - 6.0 * TIME_STEP * DIFF
 TOP = 2**BLOCKS
-BATCH = 2
+BATCH = 4
 PIECE = 1
 QUAD = 4
 ORDER = (12, 8, 4, 13, 14, 9, 5, 15, 10, 6, 11, 7, 0, 1, 2, 3)
@@ -537,7 +537,7 @@
             dma(()),
             dma((2,)),
             dma((2, pn.slots, 2)),
-            dma((pn.slots + 2, TOP // BATCH)),
+            dma((pn.slots + 2, 2 * TOP // QUAD)),
             dma(()),
             dma((pn.slots,)),
             dma(()),

time: 148 us -> 149 us (level)
  no operation moved by 1% of the time
where the time goes in v6:
time: 149 us
  Pallas kernels  147 us (99%)
  local copies, waits for them, and re-layouts  1.67 us (1%)
    pallas_call x1, Pallas kernels, local(): pl.pallas_call(partial(body, pn), out_shape=pltpu.VMEM(shape, f32), in_sp...  147 us

profile of v6, /device:TPU:9, one launch (start us, length us, event | category | flops | bytes accessed | tf_op | source)
XLA Modules:
  0.0 148.6 jit_solution(4830824432570542360)
XLA Ops:
  0.0 147.0 %exchange_evolve.1 = f32[4,16,96,128]{3,2,1,0:T(8,128)S(1)} custom-call(f32[4,16,96,128]{3,2,1,0:T(8,128)} %bitcast.4, s32[3,64]{1,0:T(4,128)} %bitcast.5, f32[8]{0:T(128)} %levels_ref.1, f32[8]{0:T(128)} %on_ref.1, f32[8]{0:T(128)} %off_ref.1, s32[4]{0:T(128)} %order_ref.1), custom_call_target="tpu_custom_call" | custom-call | tf_op jit(solution)/shard_map/exchange_evolve/pallas_call | solution.py:517
  147.0 1.7 %copy.8 = f32[64,6,16,128]{3,2,1,0:T(8,128)} copy(f32[64,6,16,128]{3,2,1,0:T(8,128)S(1)} %bitcast.3) | data formatting | bytes 6291456
